TPU v7x, 256 devices: a whole 4x4x8 slice. The times are simulated.
256 devices in a mesh: wide: 16 (over z_hi, x), narrow: 4 (over y), depth: 4 (over z_lo, core).
Axes of the slice: x: 4, y: 4, z: 8 (z_hi: 4, z_lo: 2; z = z_hi * 2 + z_lo), core: 2. Of those that a mesh axis runs over, the one named last changes fastest.
Arguments:
- patch_store: bfloat16 [64, 1024, 4096], P('wide', 'depth'), may hold values from -6 to 6
- w_key: bfloat16 [4096, 1024], P(None, 'narrow'), may hold values from -0.09375 to 0.09375
- w_value: bfloat16 [4096, 1024], P(None, 'narrow'), may hold values from -0.09375 to 0.09375
- key_gain: float32 [128], replicated, may hold values from 0.1 to 1.9
- query_gain: float32 [128], replicated, may hold values from 0.1 to 1.9
- queries: bfloat16 [256, 4096], P('wide', 'narrow'), may hold values from -6 to 6
- owner_table: int32 [64], replicated, may hold values from 0 to 63, each once
- reader_table: int32 [16, 2], replicated, may hold values from 0 to 63
- request_image: int32 [256], P('wide'), may hold values from 0 to 1
- image_tiles: int32 [64], replicated, may hold values from 1 to 4
Outputs:
- context: bfloat16 [256, 4096], P(('wide', 'depth'), 'narrow')
Inputs may be any that keep to these rules, and one draw needn't show every extreme that they name: owner_table is a permutation of the slots. `reader_table`: entries are image ids; a group's list may repeat an image.
All inputs are finite; a program needn't handle non-finite values.
Results may differ from a plain program's by a relative error of at most 0.012.
Values may be sent and summed in bfloat16 or wider, within the bound.
A program may use at most 64 MiB of HBM per device.

v0:
```python
import math

import jax
import jax.numpy as jnp
from jax import lax
from jax.sharding import PartitionSpec as P

HD = 128
TILE_P = 256


epsilon = 1e-05


def laid_out(parts, dim):
    parts = jnp.moveaxis(parts, 0, dim)
    lengths = parts.shape
    return parts.reshape(*lengths[:dim], lengths[dim] * lengths[dim + 1], *lengths[dim + 2 :])


def copy_for_each(value, axis):
    size = lax.axis_size(axis)
    return lax.all_to_all(
        jnp.broadcast_to(value[None], (size, *value.shape)), axis, 0, 0, tiled=True
    )


def gathered_copies(value, axis, dim):
    return laid_out(copy_for_each(value, axis), dim)


def in_blocks(value, dim, size):
    lengths = value.shape
    parts = value.reshape(*lengths[:dim], size, lengths[dim] // size, *lengths[dim + 1 :])
    return jnp.moveaxis(parts, dim, 0)


def summed_on_arrival(value, axis, dim):
    size = lax.axis_size(axis)
    parts = lax.all_to_all(in_blocks(value, dim, size), axis, 0, 0, tiled=True)
    return jnp.sum(parts.astype(jnp.float32), axis=0)


def sent_together(arrays, axis, dim, along):
    both = jnp.concatenate(arrays, axis=along)
    result, at, gathered = (summed_on_arrival(both, axis, dim), 0, [])
    for a in arrays:
        gathered.append(lax.slice_in_dim(result, at, at + a.shape[along], axis=along))
        at += a.shape[along]
    return tuple(gathered)


def rms_scaled(tensor, scaling):
    return tensor / jnp.sqrt(jnp.mean(tensor * tensor, axis=-1, keepdims=True) + epsilon) * scaling


def local(
    patch_store,
    w_key,
    w_value,
    key_gain,
    query_gain,
    queries,
    owner_table,
    reader_table,
    request_image,
    image_tiles,
):
    images_here, rows_here, model_width = patch_store.shape
    kv_cols = w_key.shape[1]
    kv_local = kv_cols // HD
    patch_rows = patch_store.reshape(images_here * rows_here, model_width)
    key_rows = jnp.dot(patch_rows, w_key, preferred_element_type=jnp.float32).reshape(
        images_here, rows_here, kv_local, HD
    )
    key_rows = (
        rms_scaled(key_rows, key_gain)
        .astype(jnp.bfloat16)
        .reshape(images_here, rows_here * kv_cols)
    )
    values = jnp.dot(patch_rows, w_value, preferred_element_type=jnp.float32).astype(jnp.bfloat16)
    values = values.reshape(images_here, rows_here * kv_cols)
    owner_index = lax.axis_index("wide")
    batch_here = queries.shape[0]
    group_size = queries.shape[1] // (kv_local * HD)
    normed = rms_scaled(
        queries.astype(jnp.float32).reshape(batch_here, kv_local, group_size, HD), query_gain
    ).astype(jnp.bfloat16)
    row_ids = lax.axis_index("depth") * rows_here + jnp.arange(rows_here, dtype=jnp.int32)
    scale = 1.0 / math.sqrt(HD)
    flat_normed = normed.reshape(batch_here, kv_local * group_size * HD)
    every_query, every_entry = (
        gathered_copies(flat_normed, "wide", 0),
        gathered_copies(request_image, "wide", 0),
    )
    total = every_query.shape[0]
    group_ids = jnp.arange(total, dtype=jnp.int32) // batch_here
    image_ids = reader_table[group_ids, every_entry]
    slot_ids = owner_table[image_ids]
    local_slots = owner_index * images_here + jnp.arange(images_here, dtype=jnp.int32)
    chosen = (slot_ids[:, None] == local_slots[None, :]).astype(jnp.float32)
    usable = (row_ids[None, :] // TILE_P < image_tiles[image_ids][:, None]).astype(jnp.float32)
    own_keys = key_rows.reshape(images_here, rows_here, kv_local, HD)
    own_values = values.reshape(images_here, rows_here, kv_local, HD)
    every_normed = every_query.reshape(total, kv_local, group_size, HD)
    scores = (
        jnp.einsum("bkgd,jskd->bkgjs", every_normed, own_keys, preferred_element_type=jnp.float32)
        * scale
    )
    weights = jnp.exp(scores) * chosen[:, None, None, :, None] * usable[:, None, None, None, :]
    denominator = jnp.sum(weights, axis=(3, 4)).reshape(total, kv_local * group_size)
    numerator = jnp.einsum(
        "bkgjs,jskd->bkgd",
        weights.astype(jnp.bfloat16),
        own_values,
        preferred_element_type=jnp.float32,
    )
    numerator = numerator.reshape(total, kv_local * group_size * HD)
    numerator, denominator = sent_together(
        (numerator.astype(jnp.bfloat16), denominator.astype(jnp.bfloat16)), ("wide", "depth"), 0, 1
    )
    row_count = numerator.shape[0]
    heads_here = denominator.shape[1]
    context = numerator.reshape(row_count, heads_here, HD) / denominator[:, :, None]
    return context.reshape(row_count, heads_here * HD).astype(jnp.bfloat16)


def solution(mesh):
    placed = (
        P("wide", "depth", None),
        P(None, "narrow"),
        P(None, "narrow"),
        P(),
        P(),
        P("wide", "narrow"),
        P(),
        P(),
        P("wide"),
        P(),
    )
    return jax.shard_map(
        local, mesh=mesh, in_specs=placed, out_specs=P(("wide", "depth"), "narrow"), check_vma=False
    )
```

profile of v0, /device:TPU:16, one launch (start us, length us, event | category | flops | bytes accessed | tf_op | source)
XLA Modules:
  0.0 93.2 jit_solution(358288336858850587)
XLA Ops:
  0.0 1.4 %broadcast_in_dim.5 = s32[16,1,16]{2,1,0:T(1,128)} broadcast(s32[16]{0:T(128)} %param.18), dimensions={2} | broadcast | bytes 1088 | tf_op jit(solution)/shard_map/broadcast_in_dim | solution.py:24
  1.4 11.0 %all-to-all-start.1 = ((s32[16,1,16]{2,1,0:T(1,128)}), s32[16,1,16]{2,1,0:T(1,128)S(1)}, u32[]{:S(2)}, u32[]{:S(2)}) async-start(s32[16,1,16]{2,1,0:T(1,128)} %broadcast_in_dim.5), calls=%async_computation.1 | async-start | bytes 16384 | tf_op jit(solution)/shard_map/all_to_all | solution.py:23
  12.5 4.1 %copy.54 = bf16[256,4096]{1,0:T(8,128)(2,1)} copy(bf16[256,4096]{0,1:T(8,128)(2,1)} %bitcast.51) | data formatting | bytes 4194304 | tf_op jit(solution)/shard_map/dot_general | solution.py:73
  16.6 7.4 %multiply_reduce_fusion = (f32[4,256,2]{1,2,0:T(2,128)S(1)}, f32[4,256,2,128]{1,3,2,0:T(8,128)}) fusion(bf16[2,128,4096,1]{2,1,0,3:T(8,128)(2,1)} %bitcast.52, bf16[4,256,4096]{2,1,0:T(8,128)(2,1)} %param.10), kind=kOutput, calls=%fused_computation.17 | convolution fusion | flops 2148005888 | bytes 11542528 | tf_op jit(solution)/shard_map/dot_general | solution.py:73
  24.0 0.1 reduce_sum.37
  24.2 0.1 copy.38
  24.3 0.1 copy.39
  24.4 0.1 div.69
  24.6 5.7 %convolution_convert_fusion = bf16[1024,256]{1,0:T(8,128)(2,1)S(1)} fusion(bf16[1024,4096]{1,0:T(8,128)(2,1)} %bitcast.58, bf16[4096,256]{1,0:T(8,128)(2,1)S(1)} %copy-done), kind=kOutput, calls=%fused_computation.12 | convolution fusion | flops 2147745792 | bytes 11010048 | tf_op jit(solution)/shard_map/dot_general | solution.py:81
  30.4 0.1 reshape_reshape.6
  30.5 0.8 broadcast_in_dim.4
  31.4 9.6 %all-to-all-start = ((bf16[16,16,1024]{2,1,0:T(8,128)(2,1)}), bf16[16,16,1024]{2,1,0:T(8,128)(2,1)S(1)}, u32[]{:S(2)}, u32[]{:S(2)}) async-start(bf16[16,16,1024]{2,1,0:T(8,128)(2,1)} %broadcast_in_dim.4), calls=%async_computation | async-start | bytes 1048576 | tf_op jit(solution)/shard_map/all_to_all | solution.py:23
  41.0 0.5 broadcast.236
  41.5 0.7 reduce.3
  42.2 0.1 reshape.237
  42.3 2.4 %gather_fusion = s32[256]{0:T(256)S(1)} fusion(s32[16,2]{0,1:T(2,128)S(1)} %copy-done.3, s32[256]{0:T(256)S(1)} %bitcast.50), kind=kCustom, calls=%fused_computation | custom fusion | bytes 4096 | tf_op jit(solution)/shard_map/gather | solution.py:98
  44.7 1.9 %gather_fusion.2 = s32[256]{0:T(256)S(1)} fusion(s32[64]{0:T(128)S(1)} %copy-done.1, s32[1024]{0:T(1024)S(1)} %pad_clamp_fusion), kind=kCustom, calls=%fused_computation.2 | custom fusion | bytes 3072 | tf_op jit(solution)/shard_map/gather | solution.py:102
  46.6 1.9 %gather_fusion.1 = s32[256]{0:T(256)S(1)} fusion(s32[64]{0:T(128)S(1)} %copy-done.2, s32[1024]{0:T(1024)S(1)} %pad_clamp_fusion), kind=kCustom, calls=%fused_computation.1 | custom fusion | bytes 3072 | tf_op jit(solution)/shard_map/gather | solution.py:99
  48.6 0.1 compare_convert_fusion
  48.7 8.9 %all-to-all-done = bf16[16,16,1024]{2,1,0:T(8,128)(2,1)S(1)} async-done(((bf16[16,16,1024]{2,1,0:T(8,128)(2,1)}), bf16[16,16,1024]{2,1,0:T(8,128)(2,1)S(1)}, u32[]{:S(2)}, u32[]{:S(2)}) %all-to-all-start) | async-done | bytes 524320 | tf_op jit(solution)/shard_map/all_to_all | solution.py:23
  57.6 1.2 %reshape_reshape.7 = bf16[256,2,4,128]{3,2,1,0:T(4,128)(2,1)} reshape(bf16[16,16,1024]{2,1,0:T(8,128)(2,1)S(1)} %all-to-all-done) | data formatting | bytes 1048576 | tf_op jit(solution)/shard_map/reshape;reshape | solution.py:105
  58.8 3.9 %fusion.4 = (bf16[256,2,4,4,256]{0,4,2,3,1:T(8,128)(2,1)S(1)}, bf16[256,2,4]{0,2,1:T(4,128)(2,1)S(1)}) fusion(f32[256,256]{0,1:T(8,128)S(1)} %compare_convert_fusion, f32[256,4]{0,1:T(4,128)S(1)} %compare_convert_fusion.1, bf16[256,2,4,128,1]{3,2,1,0,4:T(4,128)(2,1)} %bitcast.54, f32[128]{0:T(128)S(1)} %copy-done.6, ...), kind=kOutput, calls=%fused_computation.8 | convolution fusion | flops 548141056 | bytes 6046208 | tf_op jit(solution)/shard_map/bkgd,jskd->bkgjs/dot_general | solution.py:107
  62.6 1.6 %fusion.13 = bf16[256,2,4,128]{0,3,2,1:T(8,128)(2,1)} fusion(bf16[256,2,4,4,256]{0,4,2,3,1:T(8,128)(2,1)S(1)} %get-tuple-element.5, bf16[4,256,2,128,1]{3,2,1,0,4:T(2,128)(2,1)S(1)} %bitcast.53), kind=kOutput, calls=%fused_computation.14 | convolution fusion | flops 537133056 | bytes 5242880 | tf_op jit(solution)/shard_map/bkgjs,jskd->bkgd/dot_general | solution.py:112
  64.2 1.4 %copy.44 = bf16[256,2,4,128]{3,2,1,0:T(4,128)(2,1)S(1)} copy(bf16[256,2,4,128]{0,3,2,1:T(8,128)(2,1)} %fusion.13) | data formatting | bytes 1048576 | tf_op jit(solution)/shard_map/convert_element_type | solution.py:120
  65.6 0.1 convert_element_type.63
  65.7 0.3 convert_element_type.65
  66.0 0.5 copy.45
  66.5 0.3 pad_maximum_fusion
  66.8 25.5 %all_to_all.16 = bf16[64,4,1032]{2,1,0:T(4,128)(2,1)S(1)} all-to-all(bf16[64,4,1032]{2,1,0:T(4,128)(2,1)S(1)} %pad_maximum_fusion), channel_id=1, replica_groups=mesh['wide'=16,'narrow'=4,'depth'=4] {'wide','depth'}, dimensions={0} | all-to-all | bytes 1056768 | tf_op jit(solution)/shard_map/all_to_all | solution.py:40
  92.2 0.3 convert_reduce_fusion
  92.5 0.1 broadcast_bitcast_fusion
  92.6 0.6 fusion.23
  (29 shorter events, 0.3 us)
Async XLA Ops:
  0.0 24.6 %copy-start = (bf16[4096,256]{1,0:T(8,128)(2,1)S(1)}, bf16[4096,256]{1,0:T(8,128)(2,1)}, u32[]{:S(2)}) copy-start(bf16[4096,256]{1,0:T(8,128)(2,1)} %param.12) | copy-start | bytes 6291460
  1.4 29.1 %all-to-all-start.1 = ((s32[16,1,16]{2,1,0:T(1,128)}), s32[16,1,16]{2,1,0:T(1,128)S(1)}, u32[]{:S(2)}, u32[]{:S(2)}) async-start(s32[16,1,16]{2,1,0:T(1,128)} %broadcast_in_dim.5), calls=%async_computation.1 | async-start | bytes 16384 | tf_op jit(solution)/shard_map/all_to_all | solution.py:23
  16.6 7.4 %copy-start.4 = (bf16[16,1024]{1,0:T(8,128)(2,1)S(1)}, bf16[16,1024]{1,0:T(8,128)(2,1)}, u32[]{:S(2)}) copy-start(bf16[16,1024]{1,0:T(8,128)(2,1)} %param.15) | copy-start | bytes 98308
  16.6 7.9 %copy-start.5 = (f32[128]{0:T(128)S(1)}, f32[128]{0:T(128)}, u32[]{:S(2)}) copy-start(f32[128]{0:T(128)} %param.14) | copy-start | bytes 1540
  24.6 17.7 %copy-start.3 = (s32[16,2]{0,1:T(2,128)S(1)}, s32[16,2]{0,1:T(2,128)}, u32[]{:S(2)}) copy-start(s32[16,2]{0,1:T(2,128)} %param.17) | copy-start | bytes 388
  30.3 14.4 %copy-start.1 = (s32[64]{0:T(128)S(1)}, s32[64]{0:T(128)}, u32[]{:S(2)}) copy-start(s32[64]{0:T(128)} %param.19) | copy-start | bytes 772
  30.3 16.3 %copy-start.2 = (s32[64]{0:T(128)S(1)}, s32[64]{0:T(128)}, u32[]{:S(2)}) copy-start(s32[64]{0:T(128)} %param.16) | copy-start | bytes 772
  30.3 28.4 %copy-start.6 = (f32[128]{0:T(128)S(1)}, f32[128]{0:T(128)}, u32[]{:S(2)}) copy-start(f32[128]{0:T(128)} %param.13) | copy-start | bytes 1540
  31.4 26.3 %all-to-all-start = ((bf16[16,16,1024]{2,1,0:T(8,128)(2,1)}), bf16[16,16,1024]{2,1,0:T(8,128)(2,1)S(1)}, u32[]{:S(2)}, u32[]{:S(2)}) async-start(bf16[16,16,1024]{2,1,0:T(8,128)(2,1)} %broadcast_in_dim.4), calls=%async_computation | async-start | bytes 1048576 | tf_op jit(solution)/shard_map/all_to_all | solution.py:23
where the time goes:
time: 93.7 us; the launch traced here: 93.2 us
  blocking collectives  25.5 us (27%)
  starting transfers between devices  20.6 us (22%)
  matrix products  18.5 us (20%)
  local copies, waits for them, and re-layouts  17.1 us (18%)
  waiting for transfers between devices  8.95 us (10%)
  other arithmetic  2.23 us (2%)
    all_to_all x1, blocking collectives, summed_on_arrival(): parts = lax.all_to_all(in_blocks(value, dim, size), axis, 0, 0, tiled=True)  25.5 us
    all_to_all x2, starting transfers between devices, copy_for_each(): lax.all_to_all(jnp.broadcast_to(value[None], (size, *value.shape)), axis,...  20.6 us
    all_to_all x2, waiting for transfers between devices, copy_for_each(): lax.all_to_all(jnp.broadcast_to(value[None], (size, *value.shape)), axis,...  8.95 us
    dot_general x1, matrix products, local(): jnp.dot(patch_rows, w_key, preferred_element_type=jnp.float32)  7.35 us
    dot_general x1, matrix products, local(): jnp.dot(patch_rows, w_value, preferred_element_type=jnp.float32)  5.71 us
    dot_general x1, local copies, waits for them, and re-layouts, local(): jnp.dot(patch_rows, w_key, preferred_element_type=jnp.float32)  4.13 us
    dot_general x1, matrix products, local(): jnp.einsum('bkgd,jskd->bkgjs', every_normed, own_keys, preferred_element_...  3.86 us
    gather x1, local copies, waits for them, and re-layouts, local(): image_ids = reader_table[group_ids, every_entry]  2.41 us
  transfers between devices with their start and end apart: 2, of which 1 were waited for; matrix products, arithmetic and copies ran while one was open for 27% of the time, Pallas kernels for 0%

commit v1 on v0

v1 whole, which is shorter than its diff:
```python
import functools
import math

import jax
import jax.numpy as jnp
from jax import lax
from jax.experimental import pallas as pl
from jax.experimental.pallas import tpu as pltpu
from jax.sharding import PartitionSpec as P

HD = 128
EPS = 1e-05
NX = 4
NZH = 4
NZ = 8
SLOTS = NX * NZH
KC = 512
DEPTH = 3
MESH = pl.DeviceIdType.MESH
FAR = (2, 1, 3, 0)


def kernel(
    patches,
    w_key,
    w_value,
    key_gain,
    query_gain,
    queries,
    owner_table,
    reader_table,
    request_image,
    image_tiles,
    out,
    pbuf,
    kbuf,
    vbuf,
    acc,
    kv,
    q_norm,
    q_own,
    code_own,
    q_all,
    code_all,
    num_send,
    den_send,
    num_all,
    den_all,
    fetch_sem,
    kv_send_sem,
    kv_recv_sem,
    q_send_sem,
    q_recv_sem,
    code_send_sem,
    code_recv_sem,
    num_send_sem,
    num_recv_sem,
    den_send_sem,
    den_recv_sem,
):
    images, rows, width = patches.shape
    steps = width // KC
    heads_here = w_key.shape[1] // HD
    group_size = queries.shape[1] // w_key.shape[1]
    wide = lax.axis_index("wide")
    narrow = lax.axis_index("narrow")
    depth = lax.axis_index("depth")
    x, zh = lax.rem(wide, NX), lax.div(wide, NX)
    zl, core = lax.div(depth, 2), lax.rem(depth, 2)
    z = zh * 2 + zl

    def device(x_to, zh_to, zl_to, core_to):
        return (zh_to * NX + x_to, narrow, zl_to * 2 + core_to)

    partner = device(x, zh, zl, 1 - core)

    barrier = pltpu.get_barrier_semaphore()
    for dx in FAR:
        for dz in (4, 3, 5, 2, 6, 1, 7, 0):
            if dx or dz:
                x_to, z_to = lax.rem(x + dx, NX), lax.rem(z + dz, NZ)
                pl.semaphore_signal(
                    barrier,
                    inc=1,
                    device_id=device(x_to, lax.div(z_to, 2), lax.rem(z_to, 2), core),
                    device_id_type=MESH,
                )
    pl.semaphore_signal(barrier, inc=1, device_id=partner, device_id_type=MESH)

    def fetches(step):
        columns = pl.ds(pl.multiple_of(step * KC, KC), KC)
        return (
            pltpu.make_async_copy(patches.at[:, :, columns], pbuf.at[step], fetch_sem.at[0, step]),
            pltpu.make_async_copy(w_key.at[columns, :], kbuf.at[step], fetch_sem.at[1, step]),
            pltpu.make_async_copy(w_value.at[columns, :], vbuf.at[step], fetch_sem.at[2, step]),
        )

    for step in range(DEPTH):
        for copy in fetches(step):
            copy.start()

    mine = queries[...].astype(jnp.float32)
    gain = query_gain[...]
    for head in range(heads_here * group_size):
        part = mine[:, head * HD : (head + 1) * HD]
        mean = jnp.mean(part * part, axis=-1, keepdims=True)
        q_norm[head] = part * lax.rsqrt(mean + EPS) * gain
    for half in range(2):
        for k in range(heads_here):
            own_rows = [
                q_norm[k * group_size + g, pl.ds(8 * half + 4 * core, 4), :]
                for g in range(group_size)
            ]
            q_own[half, k] = jnp.concatenate(own_rows, axis=0).astype(jnp.bfloat16)
    lanes = lax.broadcasted_iota(jnp.int32, (1, HD), 1)
    codes = jnp.zeros((1, HD), jnp.float32)
    for half in range(2):
        for r in range(4):
            image = reader_table[wide, request_image[8 * half + 4 * core + r]]
            code = owner_table[image] * 8 + image_tiles[image]
            codes = jnp.where(lanes == half * 4 + r, code.astype(jnp.float32), codes)
    code_own[...] = codes
    q_all[0] = q_own[...]
    code_all[0] = codes

    def query_copies(d, dx):
        x_to = lax.rem(x + dx, NX)
        z_to = lax.rem(z + NZ + (2 * zl - 1) * d, NZ)
        zh_to = lax.div(z_to, 2)
        slot = dx * NZH + lax.rem(zh_to - zh + NZH, NZH)
        to = device(x_to, zh_to, lax.rem(z_to, 2), core)
        i = d * NX + dx
        return (
            pltpu.make_async_remote_copy(
                src_ref=q_own,
                dst_ref=q_all.at[slot],
                send_sem=q_send_sem.at[i],
                recv_sem=q_recv_sem.at[slot],
                device_id=to,
                device_id_type=MESH,
            ),
            pltpu.make_async_remote_copy(
                src_ref=code_own,
                dst_ref=code_all.at[slot],
                send_sem=code_send_sem.at[i],
                recv_sem=code_recv_sem.at[slot],
                device_id=to,
                device_id_type=MESH,
            ),
        )

    query_order = [(d, dx) for d in (3, 2, 1, 0) for dx in FAR if d or dx]

    def send_queries():
        pl.semaphore_wait(barrier, 2 * SLOTS)
        for d, dx in query_order:
            for copy in query_copies(d, dx):
                copy.start()

    acc[...] = jnp.zeros_like(acc)
    kv_width = heads_here * HD

    def project(step, carry):
        @pl.when(step + DEPTH < steps)
        def _():
            for copy in fetches(step + DEPTH):
                copy.start()

        for copy in fetches(step):
            copy.wait()
        block = pbuf[step].reshape(images * rows, KC)
        acc[:, :kv_width] += jnp.dot(block, kbuf[step], preferred_element_type=jnp.float32)
        acc[:, kv_width:] += jnp.dot(block, vbuf[step], preferred_element_type=jnp.float32)
        return carry

    early = steps // 2
    lax.fori_loop(0, early, project, 0)
    send_queries()
    lax.fori_loop(early, steps, project, 0)

    gain = key_gain[...]
    for k in range(heads_here):
        for j in range(images):
            raw = acc[j * rows : (j + 1) * rows, k * HD : (k + 1) * HD]
            mean = jnp.mean(raw * raw, axis=-1, keepdims=True)
            kv[core, k, 0, :, j * HD : (j + 1) * HD] = (
                raw * lax.rsqrt(mean + EPS) * gain
            ).astype(jnp.bfloat16)
            kv[core, k, 1, :, j * HD : (j + 1) * HD] = acc[
                j * rows : (j + 1) * rows, kv_width + k * HD : kv_width + (k + 1) * HD
            ].astype(jnp.bfloat16)

    def kv_copy(k):
        return pltpu.make_async_remote_copy(
            src_ref=kv.at[core, k],
            dst_ref=kv.at[core, k],
            send_sem=kv_send_sem.at[k],
            recv_sem=kv_recv_sem.at[k],
            device_id=partner,
            device_id_type=MESH,
        )

    for k in range(heads_here):
        kv_copy(k).start()

    def query_arrival(slot):
        return (
            pltpu.make_async_remote_copy(
                src_ref=q_own,
                dst_ref=q_all.at[slot],
                send_sem=q_send_sem.at[0],
                recv_sem=q_recv_sem.at[slot],
                device_id=partner,
                device_id_type=MESH,
            ),
            pltpu.make_async_remote_copy(
                src_ref=code_own,
                dst_ref=code_all.at[slot],
                send_sem=code_send_sem.at[0],
                recv_sem=code_recv_sem.at[slot],
                device_id=partner,
                device_id_type=MESH,
            ),
        )

    for slot in range(1, SLOTS):
        for copy in query_arrival(slot):
            copy.wait_recv()

    per_slot = 2 * group_size * 4
    lane = lax.broadcasted_iota(jnp.int32, (SLOTS, per_slot, HD), 2)
    row = lax.broadcasted_iota(jnp.int32, (SLOTS, per_slot, HD), 1)
    wanted = lax.div(row, 4 * group_size) * 4 + lax.rem(row, 4)
    spread = jnp.where(lane == wanted, jnp.broadcast_to(code_all[...], lane.shape), 0.0)
    total = SLOTS * per_slot
    column = jnp.sum(spread, axis=-1, keepdims=True).reshape(total, 1)
    first_slot = (wide * images * 8).astype(jnp.float32)
    local = jnp.broadcast_to(column, (total, HD)) - first_slot
    tile = (zl * 2).astype(jnp.float32)
    chosen, second = [], jnp.zeros((total, HD), jnp.float32)
    for j in range(images):
        mine_j = (local > 8.0 * j + tile) & (local < 8.0 * j + 7.0)
        chosen.append(jnp.where(mine_j, 1.0, 0.0))
        second = jnp.where((local > 8.0 * j + tile + 1.0) & (local < 8.0 * j + 7.0), 1.0, second)
    any_chosen = chosen[0]
    for j in range(1, images):
        any_chosen = any_chosen + chosen[j]
    chosen16 = [c.astype(jnp.bfloat16) for c in chosen]
    scale = 1.0 / math.sqrt(HD)

    def num_copy(slot, half, k):
        dx, dzh = slot // NZH, slot % NZH
        if slot:
            to_half = half
        else:
            to_half = 1 - zl
        to = device(lax.rem(x - dx + NX, NX), lax.rem(zh - dzh + NZH, NZH), to_half, core)
        return pltpu.make_async_remote_copy(
            src_ref=num_send.at[slot, to_half, k],
            dst_ref=num_all.at[slot * 2 + zl, k],
            send_sem=num_send_sem.at[slot * 2 + half, k],
            recv_sem=num_recv_sem.at[slot * 2 + zl, k],
            device_id=to,
            device_id_type=MESH,
        )

    def den_copy(slot, half):
        dx, dzh = slot // NZH, slot % NZH
        to_half = half if slot else 1 - zl
        to = device(lax.rem(x - dx + NX, NX), lax.rem(zh - dzh + NZH, NZH), to_half, core)
        return pltpu.make_async_remote_copy(
            src_ref=den_send.at[slot * 2 + to_half],
            dst_ref=den_all.at[slot * 2 + zl],
            send_sem=den_send_sem.at[slot * 2 + half],
            recv_sem=den_recv_sem.at[slot * 2 + zl],
            device_id=to,
            device_id_type=MESH,
        )

    return_order = [
        (dx * NZH + dzh, half)
        for dzh in FAR
        for dx in FAR
        for half in range(2 if dx or dzh else 1)
    ]

    chunk = group_size * 4
    lane3 = lax.broadcasted_iota(jnp.int32, (2 * SLOTS, chunk, HD), 2)
    row3 = lax.broadcasted_iota(jnp.int32, (2 * SLOTS, chunk, HD), 1)
    dens = jnp.zeros((2 * SLOTS, 1, HD), jnp.float32)
    for k in range(heads_here):
        kv_copy(k).wait_recv()
        q = q_all[:, :, k].reshape(total, HD)
        expanded = jnp.concatenate([q * chosen16[j] for j in range(images)], axis=-1)
        keys = kv[:, k, 0].reshape(2 * rows, images * HD)
        scores = lax.dot_general(
            expanded, keys, (((1,), (1,)), ((), ())), preferred_element_type=jnp.float32
        )
        weights = jnp.exp(scores * scale)
        w0 = weights[:, :rows]
        w1 = weights[:, rows:] * jnp.concatenate([second] * (rows // HD), axis=-1)
        both = w0 + w1
        folded = both[:, :HD]
        for i in range(1, rows // HD):
            folded = folded + both[:, i * HD : (i + 1) * HD]
        den = jnp.sum(folded, axis=-1, keepdims=True)
        values = kv[:, k, 1].reshape(2 * rows, images * HD)
        pulled = jnp.dot(
            jnp.concatenate([w0, w1], axis=-1).astype(jnp.bfloat16),
            values,
            preferred_element_type=jnp.float32,
        )
        num = pulled[:, :HD] * chosen[0]
        for j in range(1, images):
            num = num + pulled[:, j * HD : (j + 1) * HD] * chosen[j]
        num_send[:, :, k] = num.astype(jnp.bfloat16).reshape(SLOTS, 2, chunk, HD)
        for slot, half in return_order:
            num_copy(slot, half, k).start()
        den = jnp.broadcast_to(den, (total, HD)) * any_chosen
        den = den.reshape(2 * SLOTS, chunk, HD)
        dens = dens + jnp.sum(
            jnp.where(lane3 == row3 + k * chunk, den, 0.0), axis=1, keepdims=True
        )
    den_send[...] = dens
    for slot, half in return_order:
        den_copy(slot, half).start()
    num_all[zl] = num_send[0, zl]
    den_all[zl] = den_send[zl]

    for k in range(heads_here):
        for slot, half in return_order:
            pltpu.make_async_remote_copy(
                src_ref=num_send.at[slot, half, k],
                dst_ref=num_all.at[slot * 2 + (half if slot else 1 - zl), k],
                send_sem=num_send_sem.at[slot * 2 + half, k],
                recv_sem=num_recv_sem.at[slot * 2 + (half if slot else 1 - zl), k],
                device_id=partner,
                device_id_type=MESH,
            ).wait_recv()
    for slot, half in return_order:
        pltpu.make_async_remote_copy(
            src_ref=den_send.at[slot * 2 + half],
            dst_ref=den_all.at[slot * 2 + (half if slot else 1 - zl)],
            send_sem=den_send_sem.at[slot * 2 + half],
            recv_sem=den_recv_sem.at[slot * 2 + (half if slot else 1 - zl)],
            device_id=partner,
            device_id_type=MESH,
        ).wait_recv()

    den_total = jnp.sum(den_all[...], axis=0)
    pair_rows = heads_here * chunk
    lane2 = lax.broadcasted_iota(jnp.int32, (pair_rows, HD), 1)
    row2 = lax.broadcasted_iota(jnp.int32, (pair_rows, HD), 0)
    den_column = jnp.sum(
        jnp.where(lane2 == row2, jnp.broadcast_to(den_total, (pair_rows, HD)), 0.0),
        axis=-1,
        keepdims=True,
    )
    num_total = jnp.sum(num_all[...].astype(jnp.float32), axis=0).reshape(pair_rows, HD)
    context = num_total / den_column
    for head in range(heads_here * group_size):
        out[:, head * HD : (head + 1) * HD] = context[head * 4 : (head + 1) * 4, :].astype(
            jnp.bfloat16
        )

    for d, dx in query_order:
        for copy in query_copies(d, dx):
            copy.wait_send()
    for k in range(heads_here):
        kv_copy(k).wait_send()
        for slot, half in return_order:
            num_copy(slot, half, k).wait_send()
    for slot, half in return_order:
        den_copy(slot, half).wait_send()


def local(
    patch_store,
    w_key,
    w_value,
    key_gain,
    query_gain,
    queries,
    owner_table,
    reader_table,
    request_image,
    image_tiles,
):
    images, rows, width = patch_store.shape
    kv_width = w_key.shape[1]
    heads_here = kv_width // HD
    group_size = queries.shape[1] // kv_width
    batch_here = queries.shape[0]
    steps = width // KC
    chunk = group_size * 4
    vmem = pl.BlockSpec(memory_space=pltpu.VMEM)
    smem = pl.BlockSpec(memory_space=pltpu.SMEM)
    hbm = pl.BlockSpec(memory_space=pl.ANY)
    dma = pltpu.SemaphoreType.DMA
    return pl.pallas_call(
        kernel,
        out_shape=jax.ShapeDtypeStruct((4, queries.shape[1]), jnp.bfloat16),
        in_specs=[hbm] * 3 + [vmem] * 3 + [smem] * 4,
        out_specs=vmem,
        scratch_shapes=[
            pltpu.VMEM((steps, images, rows, KC), jnp.bfloat16),
            pltpu.VMEM((steps, KC, kv_width), jnp.bfloat16),
            pltpu.VMEM((steps, KC, kv_width), jnp.bfloat16),
            pltpu.VMEM((images * rows, 2 * kv_width), jnp.float32),
            pltpu.VMEM((2, heads_here, 2, rows, images * HD), jnp.bfloat16),
            pltpu.VMEM((heads_here * group_size, batch_here, HD), jnp.float32),
            pltpu.VMEM((2, heads_here, chunk, HD), jnp.bfloat16),
            pltpu.VMEM((1, HD), jnp.float32),
            pltpu.VMEM((SLOTS, 2, heads_here, chunk, HD), jnp.bfloat16),
            pltpu.VMEM((SLOTS, 1, HD), jnp.float32),
            pltpu.VMEM((SLOTS, 2, heads_here, chunk, HD), jnp.bfloat16),
            pltpu.VMEM((2 * SLOTS, 1, HD), jnp.float32),
            pltpu.VMEM((2 * SLOTS, heads_here, chunk, HD), jnp.bfloat16),
            pltpu.VMEM((2 * SLOTS, 1, HD), jnp.float32),
            dma((3, steps)),
            dma((heads_here,)),
            dma((heads_here,)),
            dma((SLOTS,)),
            dma((SLOTS,)),
            dma((SLOTS,)),
            dma((SLOTS,)),
            dma((2 * SLOTS, heads_here)),
            dma((2 * SLOTS, heads_here)),
            dma((2 * SLOTS,)),
            dma((2 * SLOTS,)),
        ],
        compiler_params=pltpu.CompilerParams(
            collective_id=0, has_side_effects=True, vmem_limit_bytes=56 * 1024 * 1024
        ),
        name="attend",
    )(
        patch_store,
        w_key,
        w_value,
        key_gain[None],
        query_gain[None],
        queries,
        owner_table,
        reader_table,
        request_image,
        image_tiles,
    )


def solution(mesh):
    placed = (
        P("wide", "depth", None),
        P(None, "narrow"),
        P(None, "narrow"),
        P(),
        P(),
        P("wide", "narrow"),
        P(),
        P(),
        P("wide"),
        P(),
    )
    return jax.shard_map(
        local, mesh=mesh, in_specs=placed, out_specs=P(("wide", "depth"), "narrow"), check_vma=False
    )
```

time: 93.7 us -> 35.8 us (0.38)
  Pallas kernels: 0 us -> 33 us
  blocking collectives: 25.5 us -> 0 us
  starting transfers between devices: 20.6 us -> 0 us
  matrix products: 18.5 us -> 0 us
  local copies, waits for them, and re-layouts: 17.1 us -> 2.65 us
  waiting for transfers between devices: 8.95 us -> 0 us
  other arithmetic: 2.23 us -> 0 us
    pallas_call x0 -> x1, Pallas kernels: none -> 33 us  [local(): pl.pallas_call(kernel, out_shape=jax.ShapeDtypeStruct((4, queries.shape[1...]
    all_to_all x1 -> x0, blocking collectives: 25.5 us -> none  [summed_on_arrival(): parts = lax.all_to_all(in_blocks(value, dim, size), axis, 0, 0, tiled=True)]
    all_to_all x2 -> x0, starting transfers between devices: 20.6 us -> none  [copy_for_each(): lax.all_to_all(jnp.broadcast_to(value[None], (size, *value.shape)), axis,...]
    dot_general x4 -> x0, matrix products: 18.5 us -> none  [the longest x1 7.35 us: local(): jnp.dot(patch_rows, w_key, preferred_element_type=jnp.float32)]
    all_to_all x2 -> x0, waiting for transfers between devices: 8.95 us -> none  [copy_for_each(): lax.all_to_all(jnp.broadcast_to(value[None], (size, *value.shape)), axis,...]
    gather x3 -> x0, local copies, waits for them, and re-layouts: 6.14 us -> none  [the longest x1 2.41 us: local(): image_ids = reader_table[group_ids, every_entry]]
    dot_general x1 -> x0, local copies, waits for them, and re-layouts: 4.13 us -> none  [local(): jnp.dot(patch_rows, w_key, preferred_element_type=jnp.float32)]
    unnamed x15 -> x2, local copies, waits for them, and re-layouts: 0.11 us -> 2.65 us
  transfers between devices with their start and end apart: 2 -> 0, of which waited for: 1 -> 0; matrix products, arithmetic and copies ran while one was open for 27% -> 0% of each run, Pallas kernels for 0% -> 0%
where the time goes in v1:
time: 35.8 us; the launch traced here: 35.6 us
  Pallas kernels  33 us (92%)
  local copies, waits for them, and re-layouts  2.65 us (7%)
    pallas_call x1, Pallas kernels, local(): pl.pallas_call(kernel, out_shape=jax.ShapeDtypeStruct((4, queries.shape[1...  33 us
    unnamed x2, local copies, waits for them, and re-layouts  2.65 us

profile of v1, /device:TPU:16, one launch (start us, length us, event | category | flops | bytes accessed | tf_op | source)
XLA Modules:
  0.0 35.6 jit_solution(10420179267136283754)
XLA Ops:
  0.0 1.4 %copy.11.reader_table = s32[16,2]{1,0:T(8,128)} copy(s32[16,2]{0,1:T(2,128)} %param.17) | data formatting | bytes 256 | tf_op args[7]
  1.4 33.0 %attend.1 = bf16[4,1024]{1,0:T(4,128)(2,1)} custom-call(bf16[4,256,4096]{2,1,0:T(8,128)(2,1)} %patches.1, bf16[4096,256]{1,0:T(8,128)(2,1)} %w_key.1, bf16[4096,256]{1,0:T(8,128)(2,1)} %w_value.1, f32[1,128]{1,0:T(1,128)} %bitcast.2, f32[1,128]{1,0:T(1,128)} %bitcast.3, bf16[16,1024]{1,0:T(8,128)(2,1)} %queries.1, s32[64]{0:T(128)} %owner_table.1, ...), custom_call_target="tpu_custom_call" | custom-call | tf_op jit(solution)/shard_map/attend/pallas_call | solution.py:400
  34.3 1.3 %copy.13 = bf16[4,1024]{1,0:T(4,128)(2,1)} copy(bf16[4,1024]{1,0:T(4,128)(2,1)} %attend.1) | data formatting | bytes 16384

commit v2 on v1

v2 whole, which is shorter than its diff:
```python
import math

import jax
import jax.numpy as jnp
from jax import lax
from jax.experimental import pallas as pl
from jax.experimental.pallas import tpu as pltpu
from jax.sharding import PartitionSpec as P

HD = 128
EPS = 1e-05
NX = 4
NZH = 4
NZ = 8
SLOTS = NX * NZH
NEAR = 3 * NX
KC = 512
WC = 1024
MESH = pl.DeviceIdType.MESH
FAR = (2, 1, 3, 0)


def kernel(
    patches,
    w_key,
    w_value,
    key_gain_in,
    query_gain_in,
    queries_in,
    owner_in,
    reader_in,
    request_in,
    tiles_in,
    out,
    pbuf,
    kbuf,
    vbuf,
    acc_k,
    acc_v,
    kv,
    queries,
    key_gain,
    query_gain,
    owner_table,
    reader_table,
    request_image,
    image_tiles,
    q_norm,
    q_own,
    code_own,
    q_all,
    code_all,
    num_send,
    den_send,
    num_all,
    den_all,
    small_sem,
    patch_sem,
    weight_sem,
    kv_sem,
    q_sem,
    code_sem,
    num_sem,
    den_sem,
):
    images, rows, width = patches.shape
    steps = width // KC
    kv_width = w_key.shape[1]
    heads_here = kv_width // HD
    group_size = queries.shape[1] // kv_width
    wide = lax.axis_index("wide")
    narrow = lax.axis_index("narrow")
    depth = lax.axis_index("depth")
    x, zh = lax.rem(wide, NX), lax.div(wide, NX)
    zl, core = lax.div(depth, 2), lax.rem(depth, 2)
    z = zh * 2 + zl

    def device(x_to, zh_to, zl_to, core_to):
        return (zh_to * NX + x_to, narrow, zl_to * 2 + core_to)

    partner = device(x, zh, zl, 1 - core)

    barrier = pltpu.get_barrier_semaphore()
    for dz in (4, 3, 5, 2, 6, 1, 7, 0):
        for dx in FAR:
            if dx or dz:
                x_to, z_to = lax.rem(x + dx, NX), lax.rem(z + dz, NZ)
                pl.semaphore_signal(
                    barrier,
                    inc=1,
                    device_id=device(x_to, lax.div(z_to, 2), lax.rem(z_to, 2), core),
                    device_id_type=MESH,
                )
    pl.semaphore_signal(barrier, inc=1, device_id=partner, device_id_type=MESH)

    small = [
        pltpu.make_async_copy(source, target, small_sem.at[i])
        for i, (source, target) in enumerate(
            (
                (queries_in, queries),
                (query_gain_in, query_gain),
                (request_in, request_image),
                (reader_in, reader_table),
                (owner_in, owner_table),
                (tiles_in, image_tiles),
                (key_gain_in, key_gain),
            )
        )
    ]
    for copy in small:
        copy.start()

    def fetch_patches(step):
        return pltpu.make_async_copy(
            patches.at[:, :, pl.ds(step * KC, KC)], pbuf.at[step], patch_sem.at[step]
        )

    def fetch_weight(which, part):
        source, target = ((w_key, kbuf), (w_value, vbuf))[which]
        span = pl.ds(part * WC, WC)
        return pltpu.make_async_copy(
            source.at[span, :], target.at[span, :], weight_sem.at[which, part]
        )

    both = steps // 2
    per = WC // KC
    fetches = []
    for step in range(steps):
        if step % per == 0:
            fetches.append([fetch_weight(0, step // per)])
            if step < both:
                fetches[-1].append(fetch_weight(1, step // per))
        else:
            fetches.append([])
        fetches[-1].append(fetch_patches(step))
    for part in range(both // per, steps // per):
        fetches[steps - 1].append(fetch_weight(1, part))

    ahead = 4
    for step in range(ahead):
        for copy in fetches[step]:
            copy.start()

    small[0].wait()
    small[1].wait()
    mine = queries[...].astype(jnp.float32)
    gain = query_gain[...]
    for head in range(heads_here * group_size):
        part = mine[:, head * HD : (head + 1) * HD]
        mean = jnp.mean(part * part, axis=-1, keepdims=True)
        q_norm[head] = part * lax.rsqrt(mean + EPS) * gain
    for half in range(2):
        for k in range(heads_here):
            own_rows = [
                q_norm[k * group_size + g, pl.ds(8 * half + 4 * core, 4), :]
                for g in range(group_size)
            ]
            q_own[half, k] = jnp.concatenate(own_rows, axis=0).astype(jnp.bfloat16)
    lanes = lax.broadcasted_iota(jnp.int32, (1, HD), 1)
    codes = jnp.zeros((1, HD), jnp.float32)
    for copy in small[2:]:
        copy.wait()
    for half in range(2):
        for r in range(4):
            image = reader_table[request_image[8 * half + 4 * core + r], wide]
            code = owner_table[image] * 8 + image_tiles[image]
            codes = jnp.where(lanes == half * 4 + r, code.astype(jnp.float32), codes)
    code_own[...] = codes
    q_all[0] = q_own[...]
    code_all[0] = codes

    def query_copies(d, dx):
        x_to = lax.rem(x + dx, NX)
        z_to = lax.rem(z + NZ + (2 * zl - 1) * d, NZ)
        zh_to = lax.div(z_to, 2)
        dzh = lax.rem(zh_to - zh + NZH, NZH)
        place = jnp.where(dzh == 2, 3, jnp.where(dzh == 3, 2, dzh))
        slot = place * NX + dx
        to = device(x_to, zh_to, lax.rem(z_to, 2), core)
        far = 1 if d == 3 else 0
        return (
            pltpu.make_async_remote_copy(
                src_ref=q_own,
                dst_ref=q_all.at[slot],
                send_sem=q_sem.at[0],
                recv_sem=q_sem.at[1 + far],
                device_id=to,
                device_id_type=MESH,
            ),
            pltpu.make_async_remote_copy(
                src_ref=code_own,
                dst_ref=code_all.at[slot],
                send_sem=code_sem.at[0],
                recv_sem=code_sem.at[1 + far],
                device_id=to,
                device_id_type=MESH,
            ),
        )

    def send_queries():
        pl.semaphore_wait(barrier, 2 * SLOTS)
        for d in (3, 2, 1, 0):
            for dx in FAR:
                if d or dx:
                    for copy in query_copies(d, dx):
                        copy.start()

    def settle(ref, sem):
        pltpu.make_async_copy(ref, ref, sem).wait()

    def project(acc, weight, step):
        block = pbuf[step].reshape(images * rows, KC)
        product = jnp.dot(
            block, weight[step * KC : (step + 1) * KC, :], preferred_element_type=jnp.float32
        )
        if step == 0:
            acc[...] = product
        else:
            acc[...] += product

    for step in range(steps):
        if step + ahead < steps:
            for copy in fetches[step + ahead]:
                copy.start()
        if step % per == 0:
            fetch_weight(0, step // per).wait()
            if step < both:
                fetch_weight(1, step // per).wait()
        fetch_patches(step).wait()
        project(acc_k, kbuf, step)
        if step < both:
            project(acc_v, vbuf, step)
        if step == 1:
            send_queries()

    def swap(which):
        return pltpu.make_async_remote_copy(
            src_ref=kv.at[which, core],
            dst_ref=kv.at[which, core],
            send_sem=kv_sem.at[which],
            recv_sem=kv_sem.at[2 + which],
            device_id=partner,
            device_id_type=MESH,
        )

    gain = key_gain[...]
    for k in range(heads_here):
        for j in range(images):
            raw = acc_k[j * rows : (j + 1) * rows, k * HD : (k + 1) * HD]
            mean = jnp.mean(raw * raw, axis=-1, keepdims=True)
            kv[0, core, k, :, j * HD : (j + 1) * HD] = (
                raw * lax.rsqrt(mean + EPS) * gain
            ).astype(jnp.bfloat16)
    swap(0).start()
    for step in range(both, steps):
        if step % per == 0:
            fetch_weight(1, step // per).wait()
        project(acc_v, vbuf, step)
    for k in range(heads_here):
        for j in range(images):
            kv[1, core, k, :, j * HD : (j + 1) * HD] = acc_v[
                j * rows : (j + 1) * rows, k * HD : (k + 1) * HD
            ].astype(jnp.bfloat16)
    swap(1).start()

    chunk = group_size * 4
    per_slot = 2 * chunk
    scale = 1.0 / math.sqrt(HD)
    first_slot = (wide * images * 8).astype(jnp.float32)
    tile = (zl * 2).astype(jnp.float32)

    def return_copies(slot, half):
        place, dx = slot // NX, slot % NX
        dzh = (0, 1, 3, 2)[place]
        to_half = half if slot else 1 - zl
        to = device(lax.rem(x - dx + NX, NX), lax.rem(zh - dzh + NZH, NZH), to_half, core)
        return (
            pltpu.make_async_remote_copy(
                src_ref=num_send.at[slot, to_half],
                dst_ref=num_all.at[slot * 2 + zl],
                send_sem=num_sem.at[0],
                recv_sem=num_sem.at[1],
                device_id=to,
                device_id_type=MESH,
            ),
            pltpu.make_async_remote_copy(
                src_ref=den_send.at[slot * 2 + to_half],
                dst_ref=den_all.at[slot * 2 + zl],
                send_sem=den_sem.at[0],
                recv_sem=den_sem.at[1],
                device_id=to,
                device_id_type=MESH,
            ),
        )

    def attend(first, last):
        count = last - first
        total = count * per_slot
        lane = lax.broadcasted_iota(jnp.int32, (count, per_slot, HD), 2)
        row = lax.broadcasted_iota(jnp.int32, (count, per_slot, HD), 1)
        wanted = lax.div(row, chunk) * 4 + lax.rem(row, 4)
        spread = jnp.where(
            lane == wanted, jnp.broadcast_to(code_all[first:last], lane.shape), 0.0
        )
        column = jnp.sum(spread, axis=-1, keepdims=True).reshape(total, 1)
        local = jnp.broadcast_to(column, (total, HD)) - first_slot
        chosen, second = [], jnp.zeros((total, HD), jnp.float32)
        for j in range(images):
            below = local < 8.0 * j + 7.0
            chosen.append(jnp.where((local > 8.0 * j + tile) & below, 1.0, 0.0))
            second = jnp.where((local > 8.0 * j + tile + 1.0) & below, 1.0, second)
        any_chosen = chosen[0]
        for j in range(1, images):
            any_chosen = any_chosen + chosen[j]
        lane3 = lax.broadcasted_iota(jnp.int32, (2 * count, chunk, HD), 2)
        row3 = lax.broadcasted_iota(jnp.int32, (2 * count, chunk, HD), 1)
        dens = jnp.zeros((2 * count, 1, HD), jnp.float32)
        all_weights = []
        for k in range(heads_here):
            q = q_all[first:last, :, k].reshape(total, HD)
            expanded = jnp.concatenate(
                [q * chosen[j].astype(jnp.bfloat16) for j in range(images)], axis=-1
            )
            if first == 0 and k == 0:
                swap(0).wait_recv()
            keys = kv[0, :, k].reshape(2 * rows, images * HD)
            scores = lax.dot_general(
                expanded, keys, (((1,), (1,)), ((), ())), preferred_element_type=jnp.float32
            )
            weights = jnp.exp(scores * scale)
            w0 = weights[:, :rows]
            w1 = weights[:, rows:] * jnp.concatenate([second] * (rows // HD), axis=-1)
            summed = w0 + w1
            folded = summed[:, :HD]
            for i in range(1, rows // HD):
                folded = folded + summed[:, i * HD : (i + 1) * HD]
            den = jnp.sum(folded, axis=-1, keepdims=True)
            den = (jnp.broadcast_to(den, (total, HD)) * any_chosen).reshape(2 * count, chunk, HD)
            dens = dens + jnp.sum(
                jnp.where(lane3 == row3 + k * chunk, den, 0.0), axis=1, keepdims=True
            )
            all_weights.append(jnp.concatenate([w0, w1], axis=-1).astype(jnp.bfloat16))
        den_send[2 * first : 2 * last] = dens
        if first == 0:
            swap(1).wait_recv()
        for k in range(heads_here):
            values = kv[1, :, k].reshape(2 * rows, images * HD)
            pulled = jnp.dot(all_weights[k], values, preferred_element_type=jnp.float32)
            num = pulled[:, :HD] * chosen[0]
            for j in range(1, images):
                num = num + pulled[:, j * HD : (j + 1) * HD] * chosen[j]
            num_send[first:last, :, k] = num.astype(jnp.bfloat16).reshape(count, 2, chunk, HD)
        for place in reversed(range(first // NX, last // NX)):
            for dx in FAR:
                slot = place * NX + dx
                for half in range(2 if slot else 1):
                    for copy in return_copies(slot, half):
                        copy.start()

    settle(q_all.at[1:NEAR], q_sem.at[1])
    settle(code_all.at[1:NEAR], code_sem.at[1])
    attend(0, NEAR)
    settle(q_all.at[NEAR:SLOTS], q_sem.at[2])
    settle(code_all.at[NEAR:SLOTS], code_sem.at[2])
    attend(NEAR, SLOTS)
    num_all[zl] = num_send[0, zl]
    den_all[zl] = den_send[zl]

    settle(q_all.at[1:SLOTS], q_sem.at[0])
    settle(code_all.at[1:SLOTS], code_sem.at[0])
    swap(0).wait_send()
    swap(1).wait_send()
    settle(num_all.at[1 : 2 * SLOTS], num_sem.at[0])
    settle(den_all.at[1 : 2 * SLOTS], den_sem.at[0])
    settle(den_all.at[1 : 2 * SLOTS], den_sem.at[1])
    settle(num_all.at[1 : 2 * SLOTS], num_sem.at[1])

    den_total = jnp.sum(den_all[...], axis=0)
    pair_rows = heads_here * chunk
    lane2 = lax.broadcasted_iota(jnp.int32, (pair_rows, HD), 1)
    row2 = lax.broadcasted_iota(jnp.int32, (pair_rows, HD), 0)
    den_column = jnp.sum(
        jnp.where(lane2 == row2, jnp.broadcast_to(den_total, (pair_rows, HD)), 0.0),
        axis=-1,
        keepdims=True,
    )
    num_total = jnp.sum(num_all[...].astype(jnp.float32), axis=0).reshape(pair_rows, HD)
    context = num_total / den_column
    for head in range(heads_here * group_size):
        out[:, head * HD : (head + 1) * HD] = context[head * 4 : (head + 1) * 4, :].astype(
            jnp.bfloat16
        )


def local(
    patch_store,
    w_key,
    w_value,
    key_gain,
    query_gain,
    queries,
    owner_table,
    reader_table,
    request_image,
    image_tiles,
):
    images, rows, width = patch_store.shape
    kv_width = w_key.shape[1]
    heads_here = kv_width // HD
    group_size = queries.shape[1] // kv_width
    steps = width // KC
    chunk = group_size * 4
    groups, reads = reader_table.shape
    vmem = pl.BlockSpec(memory_space=pltpu.VMEM)
    hbm = pl.BlockSpec(memory_space=pl.ANY)
    dma = pltpu.SemaphoreType.DMA
    return pl.pallas_call(
        kernel,
        out_shape=jax.ShapeDtypeStruct((4, queries.shape[1]), jnp.bfloat16),
        in_specs=[hbm] * 10,
        out_specs=vmem,
        scratch_shapes=[
            pltpu.VMEM((steps, images, rows, KC), jnp.bfloat16),
            pltpu.VMEM((width, kv_width), jnp.bfloat16),
            pltpu.VMEM((width, kv_width), jnp.bfloat16),
            pltpu.VMEM((images * rows, kv_width), jnp.float32),
            pltpu.VMEM((images * rows, kv_width), jnp.float32),
            pltpu.VMEM((2, 2, heads_here, rows, images * HD), jnp.bfloat16),
            pltpu.VMEM(queries.shape, jnp.bfloat16),
            pltpu.VMEM((1, HD), jnp.float32),
            pltpu.VMEM((1, HD), jnp.float32),
            pltpu.SMEM(owner_table.shape, jnp.int32),
            pltpu.SMEM((reads, groups), jnp.int32),
            pltpu.SMEM(request_image.shape, jnp.int32),
            pltpu.SMEM(image_tiles.shape, jnp.int32),
            pltpu.VMEM((heads_here * group_size, queries.shape[0], HD), jnp.float32),
            pltpu.VMEM((2, heads_here, chunk, HD), jnp.bfloat16),
            pltpu.VMEM((1, HD), jnp.float32),
            pltpu.VMEM((SLOTS, 2, heads_here, chunk, HD), jnp.bfloat16),
            pltpu.VMEM((SLOTS, 1, HD), jnp.float32),
            pltpu.VMEM((SLOTS, 2, heads_here, chunk, HD), jnp.bfloat16),
            pltpu.VMEM((2 * SLOTS, 1, HD), jnp.float32),
            pltpu.VMEM((2 * SLOTS, heads_here, chunk, HD), jnp.bfloat16),
            pltpu.VMEM((2 * SLOTS, 1, HD), jnp.float32),
            dma((7,)),
            dma((steps,)),
            dma((2, width // WC)),
            dma((4,)),
            dma((3,)),
            dma((3,)),
            dma((2,)),
            dma((2,)),
        ],
        compiler_params=pltpu.CompilerParams(
            collective_id=0, has_side_effects=True, vmem_limit_bytes=56 * 1024 * 1024
        ),
        name="attend",
    )(
        patch_store,
        w_key,
        w_value,
        key_gain[None],
        query_gain[None],
        queries,
        owner_table,
        reader_table.T,
        request_image,
        image_tiles,
    )


def solution(mesh):
    placed = (
        P("wide", "depth", None),
        P(None, "narrow"),
        P(None, "narrow"),
        P(),
        P(),
        P("wide", "narrow"),
        P(),
        P(),
        P("wide"),
        P(),
    )
    return jax.shard_map(
        local, mesh=mesh, in_specs=placed, out_specs=P(("wide", "depth"), "narrow"), check_vma=False
    )
```

time: 35.8 us -> 31.8 us (0.89)
  Pallas kernels: 33 us -> 30.3 us
  local copies, waits for them, and re-layouts: 2.65 us -> 1.3 us
    pallas_call x1, Pallas kernels: 33 us -> 30.3 us  [local(): pl.pallas_call(kernel, out_shape=jax.ShapeDtypeStruct((4, queries.shape[1...]
    unnamed x2 -> x1, local copies, waits for them, and re-layouts: 2.65 us -> 1.3 us
where the time goes in v2:
time: 31.8 us; the launch traced here: 31.6 us
  Pallas kernels  30.3 us (95%)
  local copies, waits for them, and re-layouts  1.3 us (4%)
    pallas_call x1, Pallas kernels, local(): pl.pallas_call(kernel, out_shape=jax.ShapeDtypeStruct((4, queries.shape[1...  30.3 us
    unnamed x1, local copies, waits for them, and re-layouts  1.3 us

profile of v2, /device:TPU:16, one launch (start us, length us, event | category | flops | bytes accessed | tf_op | source)
XLA Modules:
  0.0 31.6 jit_solution(14373735731000364097)
XLA Ops:
  0.0 30.3 %attend.1 = bf16[4,1024]{1,0:T(4,128)(2,1)} custom-call(bf16[4,256,4096]{2,1,0:T(8,128)(2,1)} %patches.1, bf16[4096,256]{1,0:T(8,128)(2,1)} %w_key.1, bf16[4096,256]{1,0:T(8,128)(2,1)} %w_value.1, f32[1,128]{1,0:T(1,128)} %bitcast.4, f32[1,128]{1,0:T(1,128)} %bitcast.5, bf16[16,1024]{1,0:T(8,128)(2,1)} %queries_in.1, s32[64]{0:T(128)} %owner_in.1, ...), custom_call_target="tpu_custom_call" | custom-call | tf_op jit(solution)/shard_map/attend/pallas_call | solution.py:417
  30.3 1.3 %copy.12 = bf16[4,1024]{1,0:T(4,128)(2,1)} copy(bf16[4,1024]{1,0:T(4,128)(2,1)} %attend.1) | data formatting | bytes 16384

commit v3 on v2

--- a/solution.py
+++ b/solution.py
@@ -12,12 +12,11 @@
 NX = 4
 NZH = 4
 NZ = 8
-SLOTS = NX * NZH
-NEAR = 3 * NX
+SHIFTS = (0, 1, 3, 2)
+OWN, NEAR, AWAY = (0, 1), (1, 3), (3, 4)
 KC = 512
 WC = 1024
 MESH = pl.DeviceIdType.MESH
-FAR = (2, 1, 3, 0)
 
 
 def kernel(
@@ -52,8 +51,12 @@
     code_all,
     num_send,
     den_send,
-    num_all,
-    den_all,
+    num_x,
+    den_x,
+    num_pass,
+    den_pass,
+    num_z,
+    den_z,
     small_sem,
     patch_sem,
     weight_sem,
@@ -81,16 +84,21 @@
     partner = device(x, zh, zl, 1 - core)
 
     barrier = pltpu.get_barrier_semaphore()
-    for dz in (4, 3, 5, 2, 6, 1, 7, 0):
-        for dx in FAR:
-            if dx or dz:
-                x_to, z_to = lax.rem(x + dx, NX), lax.rem(z + dz, NZ)
-                pl.semaphore_signal(
-                    barrier,
-                    inc=1,
-                    device_id=device(x_to, lax.div(z_to, 2), lax.rem(z_to, 2), core),
-                    device_id_type=MESH,
-                )
+    for dz in (4, 3, 5, 2, 6, 1, 7):
+        z_to = lax.rem(z + dz, NZ)
+        pl.semaphore_signal(
+            barrier,
+            inc=1,
+            device_id=device(x, lax.div(z_to, 2), lax.rem(z_to, 2), core),
+            device_id_type=MESH,
+        )
+    for dx in (2, 1, 3):
+        pl.semaphore_signal(
+            barrier,
+            inc=1,
+            device_id=device(lax.rem(x + dx, NX), zh, zl, core),
+            device_id_type=MESH,
+        )
     pl.semaphore_signal(barrier, inc=1, device_id=partner, device_id_type=MESH)
 
     small = [
@@ -166,44 +174,69 @@
             code = owner_table[image] * 8 + image_tiles[image]
             codes = jnp.where(lanes == half * 4 + r, code.astype(jnp.float32), codes)
     code_own[...] = codes
-    q_all[0] = q_own[...]
-    code_all[0] = codes
-
-    def query_copies(d, dx):
-        x_to = lax.rem(x + dx, NX)
-        z_to = lax.rem(z + NZ + (2 * zl - 1) * d, NZ)
-        zh_to = lax.div(z_to, 2)
-        dzh = lax.rem(zh_to - zh + NZH, NZH)
-        place = jnp.where(dzh == 2, 3, jnp.where(dzh == 3, 2, dzh))
-        slot = place * NX + dx
-        to = device(x_to, zh_to, lax.rem(z_to, 2), core)
-        far = 1 if d == 3 else 0
-        return (
+    q_all[0, 0] = q_own[...]
+    code_all[0, 0] = codes
+
+    def pair(sources, targets, send, recv, to):
+        return [
             pltpu.make_async_remote_copy(
-                src_ref=q_own,
-                dst_ref=q_all.at[slot],
-                send_sem=q_sem.at[0],
-                recv_sem=q_sem.at[1 + far],
+                src_ref=source,
+                dst_ref=target,
+                send_sem=sems.at[send],
+                recv_sem=sems.at[recv],
                 device_id=to,
                 device_id_type=MESH,
-            ),
-            pltpu.make_async_remote_copy(
-                src_ref=code_own,
-                dst_ref=code_all.at[slot],
-                send_sem=code_sem.at[0],
-                recv_sem=code_sem.at[1 + far],
-                device_id=to,
-                device_id_type=MESH,
-            ),
-        )
+            )
+            for source, target, sems in zip(sources, targets, (q_sem, code_sem))
+        ]
+
+    def start(copies):
+        for copy in copies:
+            copy.start()
 
     def send_queries():
-        pl.semaphore_wait(barrier, 2 * SLOTS)
-        for d in (3, 2, 1, 0):
-            for dx in FAR:
-                if d or dx:
-                    for copy in query_copies(d, dx):
-                        copy.start()
+        pl.semaphore_wait(barrier, NZ - 1 + NX - 1 + 1)
+        for d in (3, 2, 1):
+            z_to = lax.rem(z + NZ + (2 * zl - 1) * d, NZ)
+            zh_to = lax.div(z_to, 2)
+            dzh = lax.rem(zh_to - zh + NZH, NZH)
+            place = jnp.where(dzh == 2, 3, jnp.where(dzh == 3, 2, dzh))
+            start(
+                pair(
+                    (q_own, code_own),
+                    (q_all.at[0, place], code_all.at[0, place]),
+                    0,
+                    4 if d == 3 else 5,
+                    device(x, zh_to, lax.rem(z_to, 2), core),
+                )
+            )
+        for dx in (2, 1, 3):
+            start(
+                pair(
+                    (q_own, code_own),
+                    (q_all.at[dx, 0], code_all.at[dx, 0]),
+                    1,
+                    6,
+                    device(lax.rem(x + dx, NX), zh, zl, core),
+                )
+            )
+
+    def pass_queries(places, send, recv):
+        span = slice(*places)
+        for dx in (2, 1, 3):
+            start(
+                pair(
+                    (q_all.at[0, span], code_all.at[0, span]),
+                    (q_all.at[dx, span], code_all.at[dx, span]),
+                    send,
+                    recv,
+                    device(lax.rem(x + dx, NX), zh, zl, core),
+                )
+            )
+
+    def settle_queries(where, index):
+        settle(q_all.at[where], q_sem.at[index])
+        settle(code_all.at[where], code_sem.at[index])
 
     def settle(ref, sem):
         pltpu.make_async_copy(ref, ref, sem).wait()
@@ -269,38 +302,32 @@
     first_slot = (wide * images * 8).astype(jnp.float32)
     tile = (zl * 2).astype(jnp.float32)
 
-    def return_copies(slot, half):
-        place, dx = slot // NX, slot % NX
-        dzh = (0, 1, 3, 2)[place]
-        to_half = half if slot else 1 - zl
-        to = device(lax.rem(x - dx + NX, NX), lax.rem(zh - dzh + NZH, NZH), to_half, core)
-        return (
+    def return_pair(sources, targets, send, recv, to):
+        return [
             pltpu.make_async_remote_copy(
-                src_ref=num_send.at[slot, to_half],
-                dst_ref=num_all.at[slot * 2 + zl],
-                send_sem=num_sem.at[0],
-                recv_sem=num_sem.at[1],
+                src_ref=source,
+                dst_ref=target,
+                send_sem=sems.at[send],
+                recv_sem=sems.at[recv],
                 device_id=to,
                 device_id_type=MESH,
-            ),
-            pltpu.make_async_remote_copy(
-                src_ref=den_send.at[slot * 2 + to_half],
-                dst_ref=den_all.at[slot * 2 + zl],
-                send_sem=den_sem.at[0],
-                recv_sem=den_sem.at[1],
-                device_id=to,
-                device_id_type=MESH,
-            ),
-        )
-
-    def attend(first, last):
-        count = last - first
+            )
+            for source, target, sems in zip(sources, targets, (num_sem, den_sem))
+        ]
+
+    def settle_return(num, den, index):
+        settle(num, num_sem.at[index])
+        settle(den, den_sem.at[index])
+
+    def attend(places, index, opening):
+        span = slice(*places)
+        count = NX * (places[1] - places[0])
         total = count * per_slot
         lane = lax.broadcasted_iota(jnp.int32, (count, per_slot, HD), 2)
         row = lax.broadcasted_iota(jnp.int32, (count, per_slot, HD), 1)
         wanted = lax.div(row, chunk) * 4 + lax.rem(row, 4)
         spread = jnp.where(
-            lane == wanted, jnp.broadcast_to(code_all[first:last], lane.shape), 0.0
+            lane == wanted, jnp.broadcast_to(code_all[:, span].reshape(count, 1, HD), lane.shape), 0.0
         )
         column = jnp.sum(spread, axis=-1, keepdims=True).reshape(total, 1)
         local = jnp.broadcast_to(column, (total, HD)) - first_slot
@@ -317,11 +344,11 @@
         dens = jnp.zeros((2 * count, 1, HD), jnp.float32)
         all_weights = []
         for k in range(heads_here):
-            q = q_all[first:last, :, k].reshape(total, HD)
+            q = q_all[:, span, :, k].reshape(total, HD)
             expanded = jnp.concatenate(
                 [q * chosen[j].astype(jnp.bfloat16) for j in range(images)], axis=-1
             )
-            if first == 0 and k == 0:
+            if opening and k == 0:
                 swap(0).wait_recv()
             keys = kv[0, :, k].reshape(2 * rows, images * HD)
             scores = lax.dot_general(
@@ -340,8 +367,8 @@
                 jnp.where(lane3 == row3 + k * chunk, den, 0.0), axis=1, keepdims=True
             )
             all_weights.append(jnp.concatenate([w0, w1], axis=-1).astype(jnp.bfloat16))
-        den_send[2 * first : 2 * last] = dens
-        if first == 0:
+        den_send[:, span] = dens.reshape(NX, places[1] - places[0], 2, 1, HD)
+        if opening:
             swap(1).wait_recv()
         for k in range(heads_here):
             values = kv[1, :, k].reshape(2 * rows, images * HD)
@@ -349,33 +376,73 @@
             num = pulled[:, :HD] * chosen[0]
             for j in range(1, images):
                 num = num + pulled[:, j * HD : (j + 1) * HD] * chosen[j]
-            num_send[first:last, :, k] = num.astype(jnp.bfloat16).reshape(count, 2, chunk, HD)
-        for place in reversed(range(first // NX, last // NX)):
-            for dx in FAR:
-                slot = place * NX + dx
-                for half in range(2 if slot else 1):
-                    for copy in return_copies(slot, half):
-                        copy.start()
-
-    settle(q_all.at[1:NEAR], q_sem.at[1])
-    settle(code_all.at[1:NEAR], code_sem.at[1])
-    attend(0, NEAR)
-    settle(q_all.at[NEAR:SLOTS], q_sem.at[2])
-    settle(code_all.at[NEAR:SLOTS], code_sem.at[2])
-    attend(NEAR, SLOTS)
-    num_all[zl] = num_send[0, zl]
-    den_all[zl] = den_send[zl]
-
-    settle(q_all.at[1:SLOTS], q_sem.at[0])
-    settle(code_all.at[1:SLOTS], code_sem.at[0])
+            num_send[:, span, :, k] = num.astype(jnp.bfloat16).reshape(
+                NX, places[1] - places[0], 2, chunk, HD
+            )
+        for dx in (2, 1, 3):
+            start(
+                return_pair(
+                    (num_send.at[dx, span], den_send.at[dx, span]),
+                    (num_x.at[dx, span], den_x.at[dx, span]),
+                    index,
+                    3 + index,
+                    device(lax.rem(x - dx + NX, NX), zh, zl, core),
+                )
+            )
+
+    def pass_return(places, index):
+        span = slice(*places)
+        settle_return(num_x.at[1:NX, span], den_x.at[1:NX, span], 3 + index)
+        num = num_send[0, span].astype(jnp.float32)
+        den = den_send[0, span]
+        for dx in range(1, NX):
+            num = num + num_x[dx, span].astype(jnp.float32)
+            den = den + den_x[dx, span]
+        num_pass[span] = num.astype(jnp.bfloat16)
+        den_pass[span] = den
+        for place in range(*places):
+            for half in range(2 if place else 1):
+                to_half = half if place else 1 - zl
+                start(
+                    return_pair(
+                        (num_pass.at[place, to_half], den_pass.at[place, to_half]),
+                        (num_z.at[place * 2 + zl], den_z.at[place * 2 + zl]),
+                        6,
+                        7,
+                        device(x, lax.rem(zh - SHIFTS[place] + NZH, NZH), to_half, core),
+                    )
+                )
+
+    one_to = slice(1, NX)
+    settle_queries((0, slice(*AWAY)), 4)
+    pass_queries(AWAY, 2, 7)
+    settle_queries((0, slice(*NEAR)), 5)
+    pass_queries(NEAR, 3, 8)
+    settle_queries((one_to, slice(*OWN)), 6)
+    attend(OWN, 0, True)
+    settle_queries((one_to, slice(*AWAY)), 7)
+    attend(AWAY, 1, False)
+    settle_queries((one_to, slice(*NEAR)), 8)
+    attend(NEAR, 2, False)
+    pass_return(OWN, 0)
+    num_z[zl] = num_pass[0, zl]
+    den_z[zl] = den_pass[0, zl]
+    pass_return(AWAY, 1)
+    pass_return(NEAR, 2)
+
+    settle_queries((0, one_to), 0)
+    settle_queries((one_to, slice(*OWN)), 1)
+    settle_queries((one_to, slice(*AWAY)), 2)
+    settle_queries((one_to, slice(*NEAR)), 3)
     swap(0).wait_send()
     swap(1).wait_send()
-    settle(num_all.at[1 : 2 * SLOTS], num_sem.at[0])
-    settle(den_all.at[1 : 2 * SLOTS], den_sem.at[0])
-    settle(den_all.at[1 : 2 * SLOTS], den_sem.at[1])
-    settle(num_all.at[1 : 2 * SLOTS], num_sem.at[1])
-
-    den_total = jnp.sum(den_all[...], axis=0)
+    for index, places in enumerate((OWN, AWAY, NEAR)):
+        span = slice(*places)
+        settle_return(num_x.at[one_to, span], den_x.at[one_to, span], index)
+    settle_return(num_z.at[1:NZ], den_z.at[1:NZ], 6)
+    settle_return(num_z.at[1:NZ], den_z.at[1:NZ], 7)
+
+    den_total = jnp.sum(den_z[...], axis=0)
     pair_rows = heads_here * chunk
     lane2 = lax.broadcasted_iota(jnp.int32, (pair_rows, HD), 1)
     row2 = lax.broadcasted_iota(jnp.int32, (pair_rows, HD), 0)
@@ -384,7 +451,7 @@
         axis=-1,
         keepdims=True,
     )
-    num_total = jnp.sum(num_all[...].astype(jnp.float32), axis=0).reshape(pair_rows, HD)
+    num_total = jnp.sum(num_z[...].astype(jnp.float32), axis=0).reshape(pair_rows, HD)
     context = num_total / den_column
     for head in range(heads_here * group_size):
         out[:, head * HD : (head + 1) * HD] = context[head * 4 : (head + 1) * 4, :].astype(
@@ -436,20 +503,24 @@
             pltpu.VMEM((heads_here * group_size, queries.shape[0], HD), jnp.float32),
             pltpu.VMEM((2, heads_here, chunk, HD), jnp.bfloat16),
             pltpu.VMEM((1, HD), jnp.float32),
-            pltpu.VMEM((SLOTS, 2, heads_here, chunk, HD), jnp.bfloat16),
-            pltpu.VMEM((SLOTS, 1, HD), jnp.float32),
-            pltpu.VMEM((SLOTS, 2, heads_here, chunk, HD), jnp.bfloat16),
-            pltpu.VMEM((2 * SLOTS, 1, HD), jnp.float32),
-            pltpu.VMEM((2 * SLOTS, heads_here, chunk, HD), jnp.bfloat16),
-            pltpu.VMEM((2 * SLOTS, 1, HD), jnp.float32),
+            pltpu.VMEM((NX, NZH, 2, heads_here, chunk, HD), jnp.bfloat16),
+            pltpu.VMEM((NX, NZH, 1, HD), jnp.float32),
+            pltpu.VMEM((NX, NZH, 2, heads_here, chunk, HD), jnp.bfloat16),
+            pltpu.VMEM((NX, NZH, 2, 1, HD), jnp.float32),
+            pltpu.VMEM((NX, NZH, 2, heads_here, chunk, HD), jnp.bfloat16),
+            pltpu.VMEM((NX, NZH, 2, 1, HD), jnp.float32),
+            pltpu.VMEM((NZH, 2, heads_here, chunk, HD), jnp.bfloat16),
+            pltpu.VMEM((NZH, 2, 1, HD), jnp.float32),
+            pltpu.VMEM((NZ, heads_here, chunk, HD), jnp.bfloat16),
+            pltpu.VMEM((NZ, 1, HD), jnp.float32),
             dma((7,)),
             dma((steps,)),
             dma((2, width // WC)),
             dma((4,)),
-            dma((3,)),
-            dma((3,)),
-            dma((2,)),
-            dma((2,)),
+            dma((9,)),
+            dma((9,)),
+            dma((8,)),
+            dma((8,)),
         ],
         compiler_params=pltpu.CompilerParams(
             collective_id=0, has_side_effects=True, vmem_limit_bytes=56 * 1024 * 1024

time: 31.8 us -> 30.7 us (0.965)
  Pallas kernels: 30.3 us -> 29.3 us
    pallas_call x1, Pallas kernels: 30.3 us -> 29.3 us  [local(): pl.pallas_call(kernel, out_shape=jax.ShapeDtypeStruct((4, queries.shape[1...]
where the time goes in v3:
time: 30.7 us; the launch traced here: 30.6 us
  Pallas kernels  29.3 us (95%)
  local copies, waits for them, and re-layouts  1.3 us (4%)
    pallas_call x1, Pallas kernels, local(): pl.pallas_call(kernel, out_shape=jax.ShapeDtypeStruct((4, queries.shape[1...  29.3 us
    unnamed x1, local copies, waits for them, and re-layouts  1.3 us

profile of v3, /device:TPU:16, one launch (start us, length us, event | category | flops | bytes accessed | tf_op | source)
XLA Modules:
  0.0 30.6 jit_solution(10731329351897531039)
XLA Ops:
  0.0 29.3 %attend.1 = bf16[4,1024]{1,0:T(4,128)(2,1)} custom-call(bf16[4,256,4096]{2,1,0:T(8,128)(2,1)} %patches.1, bf16[4096,256]{1,0:T(8,128)(2,1)} %w_key.1, bf16[4096,256]{1,0:T(8,128)(2,1)} %w_value.1, f32[1,128]{1,0:T(1,128)} %bitcast.4, f32[1,128]{1,0:T(1,128)} %bitcast.5, bf16[16,1024]{1,0:T(8,128)(2,1)} %queries_in.1, s32[64]{0:T(128)} %owner_in.1, ...), custom_call_target="tpu_custom_call" | custom-call | tf_op jit(solution)/shard_map/attend/pallas_call | solution.py:484
  29.3 1.3 %copy.12 = bf16[4,1024]{1,0:T(4,128)(2,1)} copy(bf16[4,1024]{1,0:T(4,128)(2,1)} %attend.1) | data formatting | bytes 16384

commit v4 on v3

--- a/solution.py
+++ b/solution.py
@@ -15,8 +15,15 @@
 SHIFTS = (0, 1, 3, 2)
 OWN, NEAR, AWAY = (0, 1), (1, 3), (3, 4)
 KC = 512
-WC = 1024
+FIRST = 256
+AHEAD = 3
+SEND_AFTER = 1
 MESH = pl.DeviceIdType.MESH
+
+
+def steps_of(width):
+    edges = [0, FIRST, *range(2 * FIRST, width + 1, KC)]
+    return [slice(a, b) for a, b in zip(edges, edges[1:])]
 
 
 def kernel(
@@ -58,8 +65,7 @@
     num_z,
     den_z,
     small_sem,
-    patch_sem,
-    weight_sem,
+    fetch_sem,
     kv_sem,
     q_sem,
     code_sem,
@@ -67,7 +73,7 @@
     den_sem,
 ):
     images, rows, width = patches.shape
-    steps = width // KC
+    spans = steps_of(width)
     kv_width = w_key.shape[1]
     heads_here = kv_width // HD
     group_size = queries.shape[1] // kv_width
@@ -118,36 +124,25 @@
     for copy in small:
         copy.start()
 
-    def fetch_patches(step):
-        return pltpu.make_async_copy(
-            patches.at[:, :, pl.ds(step * KC, KC)], pbuf.at[step], patch_sem.at[step]
-        )
-
-    def fetch_weight(which, part):
-        source, target = ((w_key, kbuf), (w_value, vbuf))[which]
-        span = pl.ds(part * WC, WC)
-        return pltpu.make_async_copy(
-            source.at[span, :], target.at[span, :], weight_sem.at[which, part]
-        )
-
-    both = steps // 2
-    per = WC // KC
-    fetches = []
-    for step in range(steps):
-        if step % per == 0:
-            fetches.append([fetch_weight(0, step // per)])
-            if step < both:
-                fetches[-1].append(fetch_weight(1, step // per))
-        else:
-            fetches.append([])
-        fetches[-1].append(fetch_patches(step))
-    for part in range(both // per, steps // per):
-        fetches[steps - 1].append(fetch_weight(1, part))
-
-    ahead = 4
-    for step in range(ahead):
-        for copy in fetches[step]:
-            copy.start()
+    def fetch(step):
+        span = spans[step]
+        for source, target in (
+            (patches.at[:, :, span], pbuf.at[:, :, span]),
+            (w_key.at[span, :], kbuf.at[span, :]),
+            (w_value.at[span, :], vbuf.at[span, :]),
+        ):
+            pltpu.make_async_copy(source, target, fetch_sem.at[step]).start()
+
+    def settle(ref, sem):
+        pltpu.make_async_copy(ref, ref, sem).wait()
+
+    def fetched(step):
+        columns = spans[step].stop - spans[step].start
+        together = columns * (images * rows + 2 * kv_width) // kv_width
+        settle(kbuf.at[0:together, :], fetch_sem.at[step])
+
+    for step in range(AHEAD):
+        fetch(step)
 
     small[0].wait()
     small[1].wait()
@@ -238,32 +233,21 @@
         settle(q_all.at[where], q_sem.at[index])
         settle(code_all.at[where], code_sem.at[index])
 
-    def settle(ref, sem):
-        pltpu.make_async_copy(ref, ref, sem).wait()
-
-    def project(acc, weight, step):
-        block = pbuf[step].reshape(images * rows, KC)
-        product = jnp.dot(
-            block, weight[step * KC : (step + 1) * KC, :], preferred_element_type=jnp.float32
-        )
+    def project(acc, block, weight, step):
+        product = jnp.dot(block, weight[spans[step], :], preferred_element_type=jnp.float32)
         if step == 0:
             acc[...] = product
         else:
             acc[...] += product
 
-    for step in range(steps):
-        if step + ahead < steps:
-            for copy in fetches[step + ahead]:
-                copy.start()
-        if step % per == 0:
-            fetch_weight(0, step // per).wait()
-            if step < both:
-                fetch_weight(1, step // per).wait()
-        fetch_patches(step).wait()
-        project(acc_k, kbuf, step)
-        if step < both:
-            project(acc_v, vbuf, step)
-        if step == 1:
+    for step in range(len(spans)):
+        if step + AHEAD < len(spans):
+            fetch(step + AHEAD)
+        fetched(step)
+        block = pbuf[:, :, spans[step]].reshape(images * rows, -1)
+        project(acc_k, block, kbuf, step)
+        project(acc_v, block, vbuf, step)
+        if step == SEND_AFTER:
             send_queries()
 
     def swap(which):
@@ -275,26 +259,6 @@
             device_id=partner,
             device_id_type=MESH,
         )
-
-    gain = key_gain[...]
-    for k in range(heads_here):
-        for j in range(images):
-            raw = acc_k[j * rows : (j + 1) * rows, k * HD : (k + 1) * HD]
-            mean = jnp.mean(raw * raw, axis=-1, keepdims=True)
-            kv[0, core, k, :, j * HD : (j + 1) * HD] = (
-                raw * lax.rsqrt(mean + EPS) * gain
-            ).astype(jnp.bfloat16)
-    swap(0).start()
-    for step in range(both, steps):
-        if step % per == 0:
-            fetch_weight(1, step // per).wait()
-        project(acc_v, vbuf, step)
-    for k in range(heads_here):
-        for j in range(images):
-            kv[1, core, k, :, j * HD : (j + 1) * HD] = acc_v[
-                j * rows : (j + 1) * rows, k * HD : (k + 1) * HD
-            ].astype(jnp.bfloat16)
-    swap(1).start()
 
     chunk = group_size * 4
     per_slot = 2 * chunk
@@ -418,6 +382,23 @@
     pass_queries(AWAY, 2, 7)
     settle_queries((0, slice(*NEAR)), 5)
     pass_queries(NEAR, 3, 8)
+
+    gain = key_gain[...]
+    for k in range(heads_here):
+        for j in range(images):
+            raw = acc_k[j * rows : (j + 1) * rows, k * HD : (k + 1) * HD]
+            mean = jnp.mean(raw * raw, axis=-1, keepdims=True)
+            kv[0, core, k, :, j * HD : (j + 1) * HD] = (
+                raw * lax.rsqrt(mean + EPS) * gain
+            ).astype(jnp.bfloat16)
+    swap(0).start()
+    for k in range(heads_here):
+        for j in range(images):
+            kv[1, core, k, :, j * HD : (j + 1) * HD] = acc_v[
+                j * rows : (j + 1) * rows, k * HD : (k + 1) * HD
+            ].astype(jnp.bfloat16)
+    swap(1).start()
+
     settle_queries((one_to, slice(*OWN)), 6)
     attend(OWN, 0, True)
     settle_queries((one_to, slice(*AWAY)), 7)
@@ -475,7 +456,6 @@
     kv_width = w_key.shape[1]
     heads_here = kv_width // HD
     group_size = queries.shape[1] // kv_width
-    steps = width // KC
     chunk = group_size * 4
     groups, reads = reader_table.shape
     vmem = pl.BlockSpec(memory_space=pltpu.VMEM)
@@ -483,11 +463,11 @@
     dma = pltpu.SemaphoreType.DMA
     return pl.pallas_call(
         kernel,
-        out_shape=jax.ShapeDtypeStruct((4, queries.shape[1]), jnp.bfloat16),
+        out_shape=pltpu.VMEM((4, queries.shape[1]), jnp.bfloat16),
         in_specs=[hbm] * 10,
         out_specs=vmem,
         scratch_shapes=[
-            pltpu.VMEM((steps, images, rows, KC), jnp.bfloat16),
+            pltpu.VMEM(patch_store.shape, jnp.bfloat16),
             pltpu.VMEM((width, kv_width), jnp.bfloat16),
             pltpu.VMEM((width, kv_width), jnp.bfloat16),
             pltpu.VMEM((images * rows, kv_width), jnp.float32),
@@ -514,8 +494,7 @@
             pltpu.VMEM((NZ, heads_here, chunk, HD), jnp.bfloat16),
             pltpu.VMEM((NZ, 1, HD), jnp.float32),
             dma((7,)),
-            dma((steps,)),
-            dma((2, width // WC)),
+            dma((len(steps_of(width)),)),
             dma((4,)),
             dma((9,)),
             dma((9,)),

time: 30.7 us -> 26.8 us (0.87)
  Pallas kernels: 29.3 us -> 26.1 us
  local copies, waits for them, and re-layouts: 1.3 us -> 0.6 us
    pallas_call x1, Pallas kernels: 29.3 us -> 26.1 us  [local(): pl.pallas_call(kernel, out_shape=pltpu.VMEM((4, queries.shape[1]), jnp.bf...]
    unnamed x1, local copies, waits for them, and re-layouts: 1.3 us -> 0.6 us
where the time goes in v4:
time: 26.8 us; the launch traced here: 26.7 us
  Pallas kernels  26.1 us (97%)
  local copies, waits for them, and re-layouts  0.6 us (2%)
    pallas_call x1, Pallas kernels, local(): pl.pallas_call(kernel, out_shape=pltpu.VMEM((4, queries.shape[1]), jnp.bf...  26.1 us
    unnamed x1, local copies, waits for them, and re-layouts  0.6 us

profile of v4, /device:TPU:16, one launch (start us, length us, event | category | flops | bytes accessed | tf_op | source)
XLA Modules:
  0.0 26.7 jit_solution(14408988675225348175)
XLA Ops:
  0.0 26.1 %attend.1 = bf16[4,1024]{1,0:T(4,128)(2,1)S(1)} custom-call(bf16[4,256,4096]{2,1,0:T(8,128)(2,1)} %patches.1, bf16[4096,256]{1,0:T(8,128)(2,1)} %w_key.1, bf16[4096,256]{1,0:T(8,128)(2,1)} %w_value.1, f32[1,128]{1,0:T(1,128)} %bitcast.4, f32[1,128]{1,0:T(1,128)} %bitcast.5, bf16[16,1024]{1,0:T(8,128)(2,1)} %queries_in.1, s32[64]{0:T(128)} %owner_in.1, ...), custom_call_target="tpu_custom_call" | custom-call | tf_op jit(solution)/shard_map/attend/pallas_call | solution.py:464
  26.1 0.6 %copy.12 = bf16[4,1024]{1,0:T(4,128)(2,1)} copy(bf16[4,1024]{1,0:T(4,128)(2,1)S(1)} %attend.1) | data formatting | bytes 16384

commit v5 on v4

--- a/solution.py
+++ b/solution.py
@@ -64,13 +64,12 @@
     den_pass,
     num_z,
     den_z,
+    tally,
     small_sem,
     fetch_sem,
     kv_sem,
     q_sem,
-    code_sem,
     num_sem,
-    den_sem,
 ):
     images, rows, width = patches.shape
     spans = steps_of(width)
@@ -90,7 +89,7 @@
     partner = device(x, zh, zl, 1 - core)
 
     barrier = pltpu.get_barrier_semaphore()
-    for dz in (4, 3, 5, 2, 6, 1, 7):
+    for dz in (3, 5, 2, 6, 1, 7):
         z_to = lax.rem(z + dz, NZ)
         pl.semaphore_signal(
             barrier,
@@ -172,17 +171,17 @@
     q_all[0, 0] = q_own[...]
     code_all[0, 0] = codes
 
-    def pair(sources, targets, send, recv, to):
+    def pair(sources, targets, recv, to):
         return [
             pltpu.make_async_remote_copy(
                 src_ref=source,
                 dst_ref=target,
-                send_sem=sems.at[send],
-                recv_sem=sems.at[recv],
+                send_sem=q_sem.at[0],
+                recv_sem=q_sem.at[recv],
                 device_id=to,
                 device_id_type=MESH,
             )
-            for source, target, sems in zip(sources, targets, (q_sem, code_sem))
+            for source, target in zip(sources, targets)
         ]
 
     def start(copies):
@@ -190,7 +189,7 @@
             copy.start()
 
     def send_queries():
-        pl.semaphore_wait(barrier, NZ - 1 + NX - 1 + 1)
+        pl.semaphore_wait(barrier, NZ - 2 + NX - 1 + 1)
         for d in (3, 2, 1):
             z_to = lax.rem(z + NZ + (2 * zl - 1) * d, NZ)
             zh_to = lax.div(z_to, 2)
@@ -200,8 +199,7 @@
                 pair(
                     (q_own, code_own),
                     (q_all.at[0, place], code_all.at[0, place]),
-                    0,
-                    4 if d == 3 else 5,
+                    1 if d == 3 else 2,
                     device(x, zh_to, lax.rem(z_to, 2), core),
                 )
             )
@@ -210,28 +208,31 @@
                 pair(
                     (q_own, code_own),
                     (q_all.at[dx, 0], code_all.at[dx, 0]),
-                    1,
-                    6,
+                    3,
                     device(lax.rem(x + dx, NX), zh, zl, core),
                 )
             )
 
-    def pass_queries(places, send, recv):
+    def pass_queries(places, recv):
         span = slice(*places)
         for dx in (2, 1, 3):
             start(
                 pair(
                     (q_all.at[0, span], code_all.at[0, span]),
                     (q_all.at[dx, span], code_all.at[dx, span]),
-                    send,
                     recv,
                     device(lax.rem(x + dx, NX), zh, zl, core),
                 )
             )
 
-    def settle_queries(where, index):
-        settle(q_all.at[where], q_sem.at[index])
-        settle(code_all.at[where], code_sem.at[index])
+    slot_rows = 2 * heads_here * group_size * 4 // 2 + 1
+    chunk_rows = heads_here * group_size * 4 // 2 + 1
+
+    def settle_queries(slots, index):
+        settle(tally.at[0 : slots * slot_rows], q_sem.at[index])
+
+    def settle_return(chunks, index):
+        settle(tally.at[0 : chunks * chunk_rows], num_sem.at[index])
 
     def project(acc, block, weight, step):
         product = jnp.dot(block, weight[spans[step], :], preferred_element_type=jnp.float32)
@@ -266,22 +267,18 @@
     first_slot = (wide * images * 8).astype(jnp.float32)
     tile = (zl * 2).astype(jnp.float32)
 
-    def return_pair(sources, targets, send, recv, to):
+    def return_pair(sources, targets, recv, to):
         return [
             pltpu.make_async_remote_copy(
                 src_ref=source,
                 dst_ref=target,
-                send_sem=sems.at[send],
-                recv_sem=sems.at[recv],
+                send_sem=num_sem.at[0],
+                recv_sem=num_sem.at[recv],
                 device_id=to,
                 device_id_type=MESH,
             )
-            for source, target, sems in zip(sources, targets, (num_sem, den_sem))
+            for source, target in zip(sources, targets)
         ]
-
-    def settle_return(num, den, index):
-        settle(num, num_sem.at[index])
-        settle(den, den_sem.at[index])
 
     def attend(places, index, opening):
         span = slice(*places)
@@ -348,15 +345,14 @@
                 return_pair(
                     (num_send.at[dx, span], den_send.at[dx, span]),
                     (num_x.at[dx, span], den_x.at[dx, span]),
-                    index,
-                    3 + index,
+                    1 + index,
                     device(lax.rem(x - dx + NX, NX), zh, zl, core),
                 )
             )
 
     def pass_return(places, index):
         span = slice(*places)
-        settle_return(num_x.at[1:NX, span], den_x.at[1:NX, span], 3 + index)
+        settle_return((NX - 1) * 2 * (places[1] - places[0]), 1 + index)
         num = num_send[0, span].astype(jnp.float32)
         den = den_send[0, span]
         for dx in range(1, NX):
@@ -371,17 +367,15 @@
                     return_pair(
                         (num_pass.at[place, to_half], den_pass.at[place, to_half]),
                         (num_z.at[place * 2 + zl], den_z.at[place * 2 + zl]),
-                        6,
-                        7,
+                        4,
                         device(x, lax.rem(zh - SHIFTS[place] + NZH, NZH), to_half, core),
                     )
                 )
 
-    one_to = slice(1, NX)
-    settle_queries((0, slice(*AWAY)), 4)
-    pass_queries(AWAY, 2, 7)
-    settle_queries((0, slice(*NEAR)), 5)
-    pass_queries(NEAR, 3, 8)
+    settle_queries(1, 1)
+    pass_queries(AWAY, 4)
+    settle_queries(2, 2)
+    pass_queries(NEAR, 5)
 
     gain = key_gain[...]
     for k in range(heads_here):
@@ -399,11 +393,11 @@
             ].astype(jnp.bfloat16)
     swap(1).start()
 
-    settle_queries((one_to, slice(*OWN)), 6)
+    settle_queries(NX - 1, 3)
     attend(OWN, 0, True)
-    settle_queries((one_to, slice(*AWAY)), 7)
+    settle_queries(NX - 1, 4)
     attend(AWAY, 1, False)
-    settle_queries((one_to, slice(*NEAR)), 8)
+    settle_queries(2 * (NX - 1), 5)
     attend(NEAR, 2, False)
     pass_return(OWN, 0)
     num_z[zl] = num_pass[0, zl]
@@ -411,17 +405,11 @@
     pass_return(AWAY, 1)
     pass_return(NEAR, 2)
 
-    settle_queries((0, one_to), 0)
-    settle_queries((one_to, slice(*OWN)), 1)
-    settle_queries((one_to, slice(*AWAY)), 2)
-    settle_queries((one_to, slice(*NEAR)), 3)
+    settle_queries(NX * NZH - 1, 0)
     swap(0).wait_send()
     swap(1).wait_send()
-    for index, places in enumerate((OWN, AWAY, NEAR)):
-        span = slice(*places)
-        settle_return(num_x.at[one_to, span], den_x.at[one_to, span], index)
-    settle_return(num_z.at[1:NZ], den_z.at[1:NZ], 6)
-    settle_return(num_z.at[1:NZ], den_z.at[1:NZ], 7)
+    settle_return((NX - 1) * NZ + NZ - 1, 0)
+    settle_return(NZ - 1, 4)
 
     den_total = jnp.sum(den_z[...], axis=0)
     pair_rows = heads_here * chunk
@@ -493,13 +481,12 @@
             pltpu.VMEM((NZH, 2, 1, HD), jnp.float32),
             pltpu.VMEM((NZ, heads_here, chunk, HD), jnp.bfloat16),
             pltpu.VMEM((NZ, 1, HD), jnp.float32),
+            pltpu.VMEM(((NX * NZ - 1) * (heads_here * chunk // 2 + 1), 1, HD), jnp.float32),
             dma((7,)),
             dma((len(steps_of(width)),)),
             dma((4,)),
-            dma((9,)),
-            dma((9,)),
-            dma((8,)),
-            dma((8,)),
+            dma((6,)),
+            dma((5,)),
         ],
         compiler_params=pltpu.CompilerParams(
             collective_id=0, has_side_effects=True, vmem_limit_bytes=56 * 1024 * 1024

time: 26.8 us -> 26.4 us (0.985)
  Pallas kernels: 26.1 us -> 25.6 us
    pallas_call x1, Pallas kernels: 26.1 us -> 25.6 us  [local(): pl.pallas_call(kernel, out_shape=pltpu.VMEM((4, queries.shape[1]), jnp.bf...]
where the time goes in v5:
time: 26.4 us; the launch traced here: 26.2 us
  Pallas kernels  25.6 us (97%)
  local copies, waits for them, and re-layouts  0.6 us (2%)
    pallas_call x1, Pallas kernels, local(): pl.pallas_call(kernel, out_shape=pltpu.VMEM((4, queries.shape[1]), jnp.bf...  25.6 us
    unnamed x1, local copies, waits for them, and re-layouts  0.6 us

profile of v5, /device:TPU:16, one launch (start us, length us, event | category | flops | bytes accessed | tf_op | source)
XLA Modules:
  0.0 26.2 jit_solution(1331836182594465036)
XLA Ops:
  0.0 25.6 %attend.1 = bf16[4,1024]{1,0:T(4,128)(2,1)S(1)} custom-call(bf16[4,256,4096]{2,1,0:T(8,128)(2,1)} %patches.1, bf16[4096,256]{1,0:T(8,128)(2,1)} %w_key.1, bf16[4096,256]{1,0:T(8,128)(2,1)} %w_value.1, f32[1,128]{1,0:T(1,128)} %bitcast.4, f32[1,128]{1,0:T(1,128)} %bitcast.5, bf16[16,1024]{1,0:T(8,128)(2,1)} %queries_in.1, s32[64]{0:T(128)} %owner_in.1, ...), custom_call_target="tpu_custom_call" | custom-call | tf_op jit(solution)/shard_map/attend/pallas_call | solution.py:452
  25.6 0.6 %copy.12 = bf16[4,1024]{1,0:T(4,128)(2,1)} copy(bf16[4,1024]{1,0:T(4,128)(2,1)S(1)} %attend.1) | data formatting | bytes 16384

commit v6 on v5

--- a/solution.py
+++ b/solution.py
@@ -263,7 +263,7 @@
 
     chunk = group_size * 4
     per_slot = 2 * chunk
-    scale = 1.0 / math.sqrt(HD)
+    scale = 1.0 / (math.sqrt(HD) * math.log(2.0))
     first_slot = (wide * images * 8).astype(jnp.float32)
     tile = (zl * 2).astype(jnp.float32)
 
@@ -315,7 +315,7 @@
             scores = lax.dot_general(
                 expanded, keys, (((1,), (1,)), ((), ())), preferred_element_type=jnp.float32
             )
-            weights = jnp.exp(scores * scale)
+            weights = jnp.exp2(scores * scale)
             w0 = weights[:, :rows]
             w1 = weights[:, rows:] * jnp.concatenate([second] * (rows // HD), axis=-1)
             summed = w0 + w1

time: 26.4 us -> 26.3 us (level)
  no operation moved by 1% of the time
where the time goes in v6:
time: 26.3 us; the launch traced here: 26.2 us
  Pallas kernels  25.6 us (97%)
  local copies, waits for them, and re-layouts  0.6 us (2%)
    pallas_call x1, Pallas kernels, local(): pl.pallas_call(kernel, out_shape=pltpu.VMEM((4, queries.shape[1]), jnp.bf...  25.6 us
    unnamed x1, local copies, waits for them, and re-layouts  0.6 us

profile of v6, /device:TPU:16, one launch (start us, length us, event | category | flops | bytes accessed | tf_op | source)
XLA Modules:
  0.0 26.2 jit_solution(16206224116509174850)
XLA Ops:
  0.0 25.6 %attend.1 = bf16[4,1024]{1,0:T(4,128)(2,1)S(1)} custom-call(bf16[4,256,4096]{2,1,0:T(8,128)(2,1)} %patches.1, bf16[4096,256]{1,0:T(8,128)(2,1)} %w_key.1, bf16[4096,256]{1,0:T(8,128)(2,1)} %w_value.1, f32[1,128]{1,0:T(1,128)} %bitcast.4, f32[1,128]{1,0:T(1,128)} %bitcast.5, bf16[16,1024]{1,0:T(8,128)(2,1)} %queries_in.1, s32[64]{0:T(128)} %owner_in.1, ...), custom_call_target="tpu_custom_call" | custom-call | tf_op jit(solution)/shard_map/attend/pallas_call | solution.py:452
  25.6 0.6 %copy.12 = bf16[4,1024]{1,0:T(4,128)(2,1)} copy(bf16[4,1024]{1,0:T(4,128)(2,1)S(1)} %attend.1) | data formatting | bytes 16384

commit v7 on v5

--- a/solution.py
+++ b/solution.py
@@ -251,12 +251,12 @@
         if step == SEND_AFTER:
             send_queries()
 
-    def swap(which):
+    def swap(which, k):
         return pltpu.make_async_remote_copy(
-            src_ref=kv.at[which, core],
-            dst_ref=kv.at[which, core],
-            send_sem=kv_sem.at[which],
-            recv_sem=kv_sem.at[2 + which],
+            src_ref=kv.at[which, core, k],
+            dst_ref=kv.at[which, core, k],
+            send_sem=kv_sem.at[0, which, k],
+            recv_sem=kv_sem.at[1, which, k],
             device_id=partner,
             device_id_type=MESH,
         )
@@ -309,8 +309,8 @@
             expanded = jnp.concatenate(
                 [q * chosen[j].astype(jnp.bfloat16) for j in range(images)], axis=-1
             )
-            if opening and k == 0:
-                swap(0).wait_recv()
+            if opening:
+                swap(0, k).wait_recv()
             keys = kv[0, :, k].reshape(2 * rows, images * HD)
             scores = lax.dot_general(
                 expanded, keys, (((1,), (1,)), ((), ())), preferred_element_type=jnp.float32
@@ -329,9 +329,9 @@
             )
             all_weights.append(jnp.concatenate([w0, w1], axis=-1).astype(jnp.bfloat16))
         den_send[:, span] = dens.reshape(NX, places[1] - places[0], 2, 1, HD)
-        if opening:
-            swap(1).wait_recv()
         for k in range(heads_here):
+            if opening:
+                swap(1, k).wait_recv()
             values = kv[1, :, k].reshape(2 * rows, images * HD)
             pulled = jnp.dot(all_weights[k], values, preferred_element_type=jnp.float32)
             num = pulled[:, :HD] * chosen[0]
@@ -385,13 +385,13 @@
             kv[0, core, k, :, j * HD : (j + 1) * HD] = (
                 raw * lax.rsqrt(mean + EPS) * gain
             ).astype(jnp.bfloat16)
-    swap(0).start()
+        swap(0, k).start()
     for k in range(heads_here):
         for j in range(images):
             kv[1, core, k, :, j * HD : (j + 1) * HD] = acc_v[
                 j * rows : (j + 1) * rows, k * HD : (k + 1) * HD
             ].astype(jnp.bfloat16)
-    swap(1).start()
+        swap(1, k).start()
 
     settle_queries(NX - 1, 3)
     attend(OWN, 0, True)
@@ -406,8 +406,9 @@
     pass_return(NEAR, 2)
 
     settle_queries(NX * NZH - 1, 0)
-    swap(0).wait_send()
-    swap(1).wait_send()
+    for k in range(heads_here):
+        swap(0, k).wait_send()
+        swap(1, k).wait_send()
     settle_return((NX - 1) * NZ + NZ - 1, 0)
     settle_return(NZ - 1, 4)
 
@@ -484,7 +485,7 @@
             pltpu.VMEM(((NX * NZ - 1) * (heads_here * chunk // 2 + 1), 1, HD), jnp.float32),
             dma((7,)),
             dma((len(steps_of(width)),)),
-            dma((4,)),
+            dma((2, 2, heads_here)),
             dma((6,)),
             dma((5,)),
         ],

time: 26.4 us -> 26.3 us (level)
  no operation moved by 1% of the time
where the time goes in v7:
time: 26.3 us; the launch traced here: 26.2 us
  Pallas kernels  25.6 us (97%)
  local copies, waits for them, and re-layouts  0.6 us (2%)
    pallas_call x1, Pallas kernels, local(): pl.pallas_call(kernel, out_shape=pltpu.VMEM((4, queries.shape[1]), jnp.bf...  25.6 us
    unnamed x1, local copies, waits for them, and re-layouts  0.6 us

profile of v7, /device:TPU:16, one launch (start us, length us, event | category | flops | bytes accessed | tf_op | source)
XLA Modules:
  0.0 26.2 jit_solution(10378882709263757197)
XLA Ops:
  0.0 25.6 %attend.1 = bf16[4,1024]{1,0:T(4,128)(2,1)S(1)} custom-call(bf16[4,256,4096]{2,1,0:T(8,128)(2,1)} %patches.1, bf16[4096,256]{1,0:T(8,128)(2,1)} %w_key.1, bf16[4096,256]{1,0:T(8,128)(2,1)} %w_value.1, f32[1,128]{1,0:T(1,128)} %bitcast.4, f32[1,128]{1,0:T(1,128)} %bitcast.5, bf16[16,1024]{1,0:T(8,128)(2,1)} %queries_in.1, s32[64]{0:T(128)} %owner_in.1, ...), custom_call_target="tpu_custom_call" | custom-call | tf_op jit(solution)/shard_map/attend/pallas_call | solution.py:453
  25.6 0.6 %copy.12 = bf16[4,1024]{1,0:T(4,128)(2,1)} copy(bf16[4,1024]{1,0:T(4,128)(2,1)S(1)} %attend.1) | data formatting | bytes 16384
